TPU v7x, 128 devices: a whole 4x4x4 slice. The times are simulated.
128 devices in a mesh: row: 8 (over y, core), col: 16 (over x, z).
Axes of the slice: x: 4, y: 4, z: 4, core: 2. Of those that a mesh axis runs over, the one named last changes fastest.
Arguments:
- points: bfloat16 [262144, 512], P(('row', 'col')), may hold values from -6 to 6
- factor: bfloat16 [262144, 2048], P(('row', 'col')), may hold values from -0.15625 to 0.15625
- targets: bfloat16 [262144, 256], P(('row', 'col')), may hold values from -6 to 6
- pivot_slots: int32 [128, 8], P(('row', 'col')), may hold values from 0 to 2047, as said below
- pivot_counts: int32 [128], replicated, may hold values from 1 to 8, 512 in all
Outputs:
- new_columns: bfloat16 [512, 262144], P(None, ('row', 'col'))
- residual_next: float32 [262144, 256], P(('row', 'col'))
Inputs may be any that keep to these rules, and one draw needn't show every extreme that they name: `pivot_slots`: each row holds 8 different local row numbers; row d's first pivot_counts[d] entries are device d's pivots, the rest are unused. `pivot_counts`: the counts sum to 512; one of them is 8.
All inputs are finite; a program needn't handle non-finite values.
Results may differ from a plain program's by a relative error of at most 0.0029.
Values may be sent and summed in bfloat16 or wider, within the bound.
A program may use at most 128 MiB of HBM per device.

v0:
```python
import jax
import jax.numpy as jnp
from jax import lax
from jax.sharding import PartitionSpec as P

BLOCK = 512


sharpness = 1.0
ridge_shift = 0.01
damping = 1.0
epsilon = 1e-06


def joined_along(blocks, dim):
    shape = list(blocks.shape[1:])
    shape[dim] *= blocks.shape[0]
    return jnp.moveaxis(blocks, 0, dim).reshape(shape)


def sent_to_all(shard, axis):
    copies = jnp.broadcast_to(shard, (lax.axis_size(axis), *shard.shape))
    return lax.all_to_all(copies, axis, split_axis=0, concat_axis=0, tiled=True)


def collect(shard, axis, dim):
    return joined_along(sent_to_all(shard, axis), dim)


def side_by_side(arrays, axis, dim, along):
    widths = [a.shape[along] for a in arrays]
    both = jnp.concatenate(arrays, axis=along)
    out = collect(both, axis, dim)
    return tuple(jnp.split(out, [sum(widths[:k]) for k in range(1, len(widths))], axis=along))


def side_by_side_2(arrays, axis, dim, along):
    both = jnp.concatenate(arrays, axis=along)
    out, at, finished = (lax.all_gather(both, axis, axis=dim, tiled=True), 0, [])
    for a in arrays:
        finished.append(lax.slice_in_dim(out, at, at + a.shape[along], axis=along))
        at += a.shape[along]
    return tuple(finished)


def normalize(points):
    values = points.astype(jnp.float32)
    factor_scale = lax.rsqrt(jnp.mean(values * values, axis=1, keepdims=True) + epsilon)
    return (values * factor_scale).astype(jnp.bfloat16)


def kernel(left_rows, right_rows, feature_width):
    cosine = (
        lax.dot_general(
            left_rows, right_rows, (((1,), (1,)), ((), ())), preferred_element_type=jnp.float32
        )
        / feature_width
    )
    return jnp.exp(sharpness * (cosine - 1.0))


def compact_index(pivot_counts, block_size):
    owners_count = pivot_counts.shape[0]
    run_ends = jnp.cumsum(pivot_counts)
    run_starts = run_ends - pivot_counts
    position = jnp.arange(block_size, dtype=jnp.int32)
    owners = jnp.sum((position[:, None] >= run_ends[None, :]).astype(jnp.int32), axis=1)
    onehot = (owners[:, None] == jnp.arange(owners_count, dtype=jnp.int32)[None, :]).astype(
        jnp.int32
    )
    first_row = jnp.sum(onehot * run_starts[None, :], axis=1)
    return (owners, position - first_row)


def block_factor(pivot_scaled, pivot_factor):
    intersection = lax.dot_general(
        pivot_factor, pivot_factor, (((1,), (1,)), ((), ())), preferred_element_type=jnp.float32
    )
    diag_shift = ridge_shift + jnp.max(jnp.sum(jnp.abs(intersection), axis=1))
    ridged = (
        kernel(pivot_scaled, pivot_scaled, pivot_scaled.shape[1])
        - intersection
        + diag_shift * jnp.eye(intersection.shape[0], dtype=jnp.float32)
    )
    return jnp.linalg.cholesky(ridged)


def on_device(points, factor, targets, pivot_slots, pivot_counts):
    scaled = normalize(points)
    local_slots = pivot_slots[0]
    slot_cap = pivot_slots.shape[1]
    own_scaled = jnp.take(scaled, local_slots, axis=0)
    own_factor = jnp.take(factor, local_slots, axis=0)
    inner_scaled, inner_factor = side_by_side((own_scaled, own_factor), "col", 0, 1)
    padded_scaled, padded_factor = side_by_side_2((inner_scaled, inner_factor), "row", 0, 1)
    owners, slot_index = compact_index(pivot_counts, BLOCK)
    row_index = owners * slot_cap + slot_index
    pivot_scaled = jnp.take(padded_scaled, row_index, axis=0)
    pivot_factor = jnp.take(padded_factor, row_index, axis=0)
    lower_factor = block_factor(pivot_scaled, pivot_factor)
    downdated = kernel(pivot_scaled, scaled, scaled.shape[1]) - lax.dot_general(
        pivot_factor, factor, (((1,), (1,)), ((), ())), preferred_element_type=jnp.float32
    )
    new_columns = lax.linalg.triangular_solve(
        lower_factor, downdated, left_side=True, lower=True
    ).astype(jnp.bfloat16)
    cross_terms = jnp.concatenate(
        [
            lax.dot_general(
                factor, targets, (((0,), (0,)), ((), ())), preferred_element_type=jnp.float32
            ),
            lax.dot_general(
                new_columns, targets, (((1,), (0,)), ((), ())), preferred_element_type=jnp.float32
            ),
        ],
        axis=0,
    )
    col_norms = jnp.concatenate(
        [
            jnp.sum(jnp.square(factor.astype(jnp.float32)), axis=0),
            jnp.sum(jnp.square(new_columns.astype(jnp.float32)), axis=1),
        ],
        axis=0,
    )
    cross_whole, norm_whole = lax.psum((cross_terms, col_norms), ("row", "col"))
    coefficients = (cross_whole / (norm_whole + damping)[:, None]).astype(jnp.bfloat16)
    held_count = factor.shape[1]
    fitted = jnp.dot(factor, coefficients[:held_count], preferred_element_type=jnp.float32)
    fitted = fitted + lax.dot_general(
        new_columns,
        coefficients[held_count:],
        (((0,), (0,)), ((), ())),
        preferred_element_type=jnp.float32,
    )
    residual_next = targets.astype(jnp.float32) - fitted
    return (new_columns, residual_next)


def solution(mesh):
    return jax.shard_map(
        on_device,
        mesh=mesh,
        in_specs=(
            P(("row", "col"), None),
            P(("row", "col"), None),
            P(("row", "col"), None),
            P(("row", "col"), None),
            P(),
        ),
        out_specs=(P(None, ("row", "col")), P(("row", "col"), None)),
        check_vma=False,
    )
```

profile of v0, /device:TPU:1, one launch (start us, length us, event | category | flops | bytes accessed | tf_op | source)
XLA Modules:
  0.0 445.7 jit_solution(6333423315457462046)
XLA Ops:
  7.2 0.8 fusion.40
  8.0 0.7 compare_and_fusion
  8.7 2.1 fusion
  11.3 0.6 gather_fusion
  11.9 5.1 %gather_fusion.1 = bf16[8,2048]{1,0:T(8,128)(2,1)S(1)} fusion(bf16[2048,2048]{1,0:T(8,128)(2,1)} %param.6, s32[1024]{0:T(1024)S(1)} %pad_clamp_fusion.1), kind=kCustom, calls=%fused_computation.1 | custom fusion | bytes 65568 | tf_op jit(solution)/shard_map/jit(_take)/gather | solution.py:93
  17.1 20.0 %all_to_all.5 = bf16[16,8,2560]{2,1,0:T(8,128)(2,1)} all-to-all(bf16[16,8,2560]{2,1,0:T(8,128)(2,1)S(1)} %broadcast_in_dim.57), channel_id=1, replica_groups=mesh['row'=8,'col'=16] {'col'}, dimensions={0} | all-to-all | bytes 1310720 | tf_op jit(solution)/shard_map/all_to_all | solution.py:23
  38.6 7.2 %fusion.51 = f32[2048,256]{1,0:T(8,128)} fusion(bf16[2048,2048]{1,0:T(8,128)(2,1)} %param.6, bf16[2048,256]{1,0:T(8,128)(2,1)S(1)} %copy-done.6), kind=kOutput, calls=%fused_computation.123 | convolution fusion | flops 2147483648 | bytes 11534336 | tf_op jit(solution)/shard_map/dot_general | solution.py:109
  45.8 27.9 %all-gather.2.cloned.1.call-done = bf16[1024,2560]{1,0:T(8,128)(2,1)} async-done(((bf16[128,2560]{1,0:T(8,128)(2,1)}), bf16[1024,2560]{1,0:T(8,128)(2,1)}) %all-gather.2.cloned.1.call-update) | async-done | bytes 5242896 | tf_op jit(solution)/shard_map/all_gather | solution.py:39
  73.7 4.8 %slice.140 = bf16[1024,2048]{1,0:T(8,128)(2,1)} slice(bf16[1024,2560]{1,0:T(8,128)(2,1)} %all-gather.2.cloned.1.call-done), slice={[0:1024], [512:2560]} | slice | bytes 8388608 | tf_op jit(solution)/shard_map/slice | solution.py:41
  78.5 8.0 %gather_fusion.3 = bf16[512,2048]{1,0:T(8,128)(2,1)} fusion(bf16[1024,2048]{1,0:T(8,128)(2,1)} %slice.140, s32[1024]{0:T(1024)S(1)} %pad_clamp_fusion), kind=kCustom, calls=%fused_computation.3 | custom fusion | bytes 4196352 | tf_op jit(solution)/shard_map/jit(_take)/gather | solution.py:99
  86.4 4.7 %abs_reduce_fusion = (f32[512]{0:T(512)S(1)}, f32[512,512]{0,1:T(8,128)}) fusion(bf16[512,2048]{1,0:T(8,128)(2,1)} %gather_fusion.3, pred[512]{0:T(512)(128)(4,1)S(1)} %compare_and_fusion.1), kind=kOutput, calls=%fused_computation.48 | convolution fusion | flops 1075314176 | bytes 3148288 | tf_op jit(solution)/shard_map/dot_general | solution.py:76
  91.1 9.7 %fusion.21 = f32[512,2048]{1,0:T(8,128)} fusion(bf16[2048,2048]{1,0:T(8,128)(2,1)} %param.6, bf16[512,2048]{1,0:T(8,128)(2,1)S(1)} %copy-done.4, pred[512]{0:T(512)(128)(4,1)S(1)} %compare_and_fusion.1), kind=kOutput, calls=%fused_computation.51 | convolution fusion | flops 4296015872 | bytes 14680576 | tf_op jit(solution)/shard_map/dot_general | solution.py:101
  100.9 2.6 copy.20
  103.5 2.8 gather_fusion.2
  106.3 2.1 fusion.17
  108.4 1.3 copy.21
  109.7 0.7 reduce_max.9
  111.1 1.4 add_multiply_fusion
  112.6 1.0 copy-done.3
  113.5 11.7 %cholesky.103 = f32[128,128]{1,0:T(8,128)S(1)} custom-call(f32[128,128]{1,0:T(8,128)S(1)} %cholesky.263), custom_call_target="Cholesky" | custom-call | tf_op jit(solution)/shard_map/jit(cholesky)/cholesky | solution.py:85
  125.4 9.8 %custom-call.30 = f32[1,128,128]{1,2,0:T(8,128)S(1)} custom-call(f32[1,128,128]{2,1,0:T(8,128)S(1)} %get-tuple-element.37), custom_call_target="InvertDiagBlocksLowerTriangular" | custom-call | tf_op jit(solution)/shard_map/jit(cholesky)/cholesky | solution.py:85
  135.2 1.2 constant_dynamic-update-slice_fusion.3
  136.5 1.3 convolution_subtract_fusion.2
  137.8 11.7 %cholesky.215 = f32[128,128]{1,0:T(8,128)S(1)} custom-call(f32[128,128]{1,0:T(8,128)S(1)} %cholesky.267), custom_call_target="Cholesky" | custom-call | tf_op jit(solution)/shard_map/jit(cholesky)/cholesky | solution.py:85
  149.5 10.0 %custom-call.31 = f32[1,128,128]{1,2,0:T(8,128)S(1)} custom-call(f32[1,128,128]{2,1,0:T(8,128)S(1)} %get-tuple-element.34), custom_call_target="InvertDiagBlocksLowerTriangular" | custom-call | tf_op jit(solution)/shard_map/jit(cholesky)/cholesky | solution.py:85
  159.8 1.3 convolution_subtract_fusion.3
  161.1 11.7 %cholesky.236 = f32[128,128]{1,0:T(8,128)S(1)} custom-call(f32[128,128]{1,0:T(8,128)S(1)} %cholesky.272), custom_call_target="Cholesky" | custom-call | tf_op jit(solution)/shard_map/jit(cholesky)/cholesky | solution.py:85
  172.8 0.7 compare_reduce_fusion.1
  173.5 9.8 %custom-call.32 = f32[1,128,128]{1,2,0:T(8,128)S(1)} custom-call(f32[1,128,128]{2,1,0:T(8,128)S(1)} %get-tuple-element.31), custom_call_target="InvertDiagBlocksLowerTriangular" | custom-call | tf_op jit(solution)/shard_map/jit(cholesky)/cholesky | solution.py:85
  183.6 1.2 convolution_subtract_fusion.4
  184.8 12.1 %cholesky.253 = f32[128,128]{1,0:T(8,128)S(1)} custom-call(f32[128,128]{1,0:T(8,128)S(1)} %convolution_subtract_fusion.4), custom_call_target="Cholesky" | custom-call | tf_op jit(solution)/shard_map/jit(cholesky)/cholesky | solution.py:85
  196.9 0.6 compare_reduce_fusion
  197.5 0.7 compare_reduce_fusion.2
  200.7 1.1 select_select_fusion
  201.8 14.1 %while.1 = (s32[]{:T(128)}, f32[512,512]{1,0:T(8,128)}, s32[4,2]{0,1:T(2,128)S(1)}, f32[4,128,128]{2,1,0:T(8,128)}, s32[]{:T(128)}) while((s32[]{:T(128)}, f32[512,512]{1,0:T(8,128)}, s32[4,2]{0,1:T(2,128)S(1)}, f32[4,128,128]{2,1,0:T(8,128)}, s32[]{:T(128)}) %tuple.39), condition=%wide.while_cond, body=%wide.while_body.sunk | while | flops 2 | bytes 132705 | solution.py:104
  201.9 0.6 fusion.67
  202.5 2.9 bitcast_dynamic-update-slice_fusion.2
  205.5 0.6 fusion.67
  206.1 2.9 bitcast_dynamic-update-slice_fusion.2
  209.0 0.6 fusion.67
  209.6 2.9 bitcast_dynamic-update-slice_fusion.2
  212.5 0.6 fusion.67
  213.1 2.8 bitcast_dynamic-update-slice_fusion.2
  216.0 40.1 %custom-call.33 = f32[4,128,128]{1,2,0:T(8,128)S(1)} custom-call(f32[4,128,128]{2,1,0:T(8,128)} %get-tuple-element.9), custom_call_target="InvertDiagBlocksLowerTriangular" | custom-call | tf_op jit(solution)/shard_map/triangular_solve | solution.py:104
  256.1 3.7 exponential_subtract_fusion
  259.8 1.1 fusion.50
  260.9 1.9 convolution_subtract_fusion.1
  262.8 1.0 fusion.49
  263.8 2.2 convolution_subtract_fusion
  266.0 1.0 fusion.48
  267.1 3.0 fusion.9
  270.1 1.1 convolution_convert_fusion
  271.1 0.8 multiply_reduce_fusion.1
  271.9 1.3 copy-done
  273.2 0.7 fusion.52
  274.3 1.7 pad_maximum_fusion
  276.0 0.6 copy.22
  276.7 5.1 %multiply_reduce_fusion = f32[2048]{0:T(1024)S(1)} fusion(bf16[2048,2048]{1,0:T(8,128)(2,1)} %param.6), kind=kLoop, calls=%fused_computation.6 | loop fusion | flops 12580864 | bytes 8396800 | tf_op jit(solution)/shard_map/reduce_sum | solution.py:120
  281.8 65.6 %psum.15 = f32[2560]{0:T(1024)S(1)} all-reduce(f32[2560]{0:T(1024)S(1)} %pad_maximum_fusion.3), channel_id=1, replica_groups=mesh['row'=8,'col'=16] {'row','col'}, use_global_device_ids=true, to_apply=%region_17.18 | all-reduce | flops 2560 | bytes 20480 | tf_op jit(solution)/shard_map/psum | solution.py:125
  347.4 80.7 %all-reduce.3.cloned.1.call-done = f32[2560,256]{1,0:T(8,128)} async-done(((f32[2560,256]{1,0:T(8,128)}), f32[2560,256]{1,0:T(8,128)}) %all-reduce.3.cloned.1.call-update) | async-done | bytes 2621456 | tf_op jit(solution)/shard_map/psum | solution.py:125
  428.0 2.1 divide_convert_fusion
  430.2 5.9 %convolution_bitcast_fusion = f32[2048,256]{0,1:T(8,128)S(1)} fusion(bf16[2048,2048]{1,0:T(8,128)(2,1)} %param.6, bf16[2560,256]{1,0:T(8,128)(2,1)S(1)} %divide_convert_fusion), kind=kOutput, calls=%fused_computation.21 | convolution fusion | flops 2147483648 | bytes 11534336 | tf_op jit(solution)/shard_map/dot_general | solution.py:128
  436.1 0.8 fusion.8
  436.9 1.8 copy.24
  (58 shorter events, 3.5 us)
Async XLA Ops:
  7.2 66.5 %all-gather.2.cloned.1.call-start = ((), (), s32[]{:S(2)}) async-start(), calls=%async_computation.1 | async-start | bytes 5898240 | tf_op jit(solution)/shard_map/all_gather | solution.py:39
  7.2 3.6 copy-start.2
  11.3 26.5 %copy-start.8 = (s32[128]{0:T(128)S(1)}, s32[128]{0:T(128)}, u32[]{:S(2)}) copy-start(s32[128]{0:T(128)} %param.9) | copy-start | bytes 1540
  11.3 27.4 %copy-start.6 = (bf16[2048,256]{1,0:T(8,128)(2,1)S(1)}, bf16[2048,256]{1,0:T(8,128)(2,1)}, u32[]{:S(2)}) copy-start(bf16[2048,256]{1,0:T(8,128)(2,1)} %param.7) | copy-start | bytes 3145732
  37.2 390.8 %all-reduce.3.cloned.1.call-start = ((), (), s32[]{:S(2)}) async-start(), calls=%async_computation.2 | async-start | bytes 5242880 | tf_op jit(solution)/shard_map/psum | solution.py:125
  86.4 4.7 %copy-start.4 = (bf16[512,2048]{1,0:T(8,128)(2,1)S(1)}, bf16[512,2048]{1,0:T(8,128)(2,1)}, u32[]{:S(2)}) copy-start(bf16[512,2048]{1,0:T(8,128)(2,1)} %gather_fusion.3) | copy-start | bytes 6291460
  100.9 2.6 slice-start
  112.5 1.0 copy-start.3
  270.1 3.2 copy-start.7
  271.9 1.3 copy-start
  271.9 2.3 copy-start.5
  430.2 5.9 %copy-start.1 = (bf16[512,2048]{1,0:T(8,128)(2,1)S(1)}, bf16[512,2048]{1,0:T(8,128)(2,1)}, u32[]{:S(2)}) copy-start(bf16[512,2048]{1,0:T(8,128)(2,1)} %copy-done) | copy-start | bytes 6291460
Sparse Core Ops, SparseCore 0:
  37.3 36.3 all-gather.1
  276.1 151.8 all-reduce.2
where the time goes:
time: 450 us; the launch traced here: 446 us
  other arithmetic  137 us (30%)
  waiting for transfers between devices  109 us (24%)
  blocking collectives  85.6 us (19%)
  matrix products  51.6 us (11%)
  local copies, waits for them, and re-layouts  44.5 us (10%)
  between operations  17.9 us (4%)
    psum x1, waiting for transfers between devices, on_device(): cross_whole, norm_whole = lax.psum((cross_terms, col_norms), ('row', 'col'))  80.7 us
    another operation x14, other arithmetic, block_factor(): return jnp.linalg.cholesky(ridged)  79 us
    psum x1, blocking collectives, on_device(): cross_whole, norm_whole = lax.psum((cross_terms, col_norms), ('row', 'col'))  65.6 us
    another operation x3, other arithmetic, on_device(): lax.linalg.triangular_solve(lower_factor, downdated, left_side=True, lowe...  41.2 us
    all_gather x1, waiting for transfers between devices, side_by_side_2(): lax.all_gather(both, axis, axis=dim, tiled=True)  27.9 us
    all_to_all x1, blocking collectives, sent_to_all(): return lax.all_to_all(copies, axis, split_axis=0, concat_axis=0, tiled=True)  20 us
    another operation x13, local copies, waits for them, and re-layouts  14.2 us
    another operation x7, matrix products, on_device(): lax.linalg.triangular_solve(lower_factor, downdated, left_side=True, lowe...  11.3 us
  transfers between devices with their start and end apart: 2, of which 2 were waited for; matrix products, arithmetic and copies ran while one was open for 3% of the time, Pallas kernels for 0%

commit v1 on v0

v1 whole, which is shorter than its diff:
```python
import functools

import jax
import jax.numpy as jnp
from jax import lax
from jax.experimental import pallas as pl
from jax.experimental.pallas import tpu as pltpu
from jax.sharding import PartitionSpec as P

BLOCK = 512
PANEL = 128
SUB = 8
TILE_PTS = 512
MESH = pl.DeviceIdType.MESH
HIGHEST = lax.Precision.HIGHEST

ridge_shift = 0.01
damping = 1.0
epsilon = 1e-06


def joined_along(blocks, dim):
    shape = list(blocks.shape[1:])
    shape[dim] *= blocks.shape[0]
    return jnp.moveaxis(blocks, 0, dim).reshape(shape)


def sent_to_all(shard, axis):
    copies = jnp.broadcast_to(shard, (lax.axis_size(axis), *shard.shape))
    return lax.all_to_all(copies, axis, split_axis=0, concat_axis=0, tiled=True)


def normalize(points):
    values = points.astype(jnp.float32)
    factor_scale = lax.rsqrt(jnp.mean(values * values, axis=1, keepdims=True) + epsilon)
    return (values * factor_scale).astype(jnp.bfloat16)


def compact_index(pivot_counts, block_size):
    owners_count = pivot_counts.shape[0]
    run_ends = jnp.cumsum(pivot_counts).astype(jnp.int32)
    run_starts = (run_ends - pivot_counts).astype(jnp.int32)
    position = jnp.arange(block_size, dtype=jnp.int32)
    owners = jnp.sum((position[:, None] >= run_ends[None, :]).astype(jnp.int32), axis=1)
    owners = owners.astype(jnp.int32)
    onehot = (owners[:, None] == jnp.arange(owners_count, dtype=jnp.int32)[None, :]).astype(
        jnp.int32
    )
    first_row = jnp.sum(onehot * run_starts[None, :], axis=1)
    return (owners, position - first_row)


def dot_nt(a, b):
    return lax.dot_general(a, b, (((1,), (1,)), ((), ())), preferred_element_type=jnp.float32)


def dot_nn(a, b):
    return jnp.dot(a, b, preferred_element_type=jnp.float32)


def panel_inverse(block):
    groups = PANEL // SUB
    sub = lax.broadcasted_iota(jnp.int32, (SUB, PANEL), 0)
    lane = lax.broadcasted_iota(jnp.int32, (SUB, PANEL), 1)
    rows = [block[SUB * r : SUB * (r + 1), :] for r in range(groups)]
    inv = [(lane == sub + SUB * r).astype(jnp.float32) for r in range(groups)]

    def over_sublanes(value, k):
        return jnp.broadcast_to(value[k : k + 1, :], (SUB, PANEL))

    for m in range(groups):
        live = range(m, groups)
        cols = {
            (r, k): jnp.broadcast_to(
                rows[r][:, SUB * m + k : SUB * m + k + 1], (SUB, PANEL)
            )
            for r in live
            for k in range(SUB)
        }
        pivots = jnp.ones((SUB, PANEL), jnp.float32)
        for k in range(SUB):
            pivot = over_sublanes(cols[m, k], k)
            pivots = jnp.where(sub == k, pivot, pivots)
            scale = 1.0 / pivot
            ahead = {j: over_sublanes(cols[m, j], k) for j in range(k + 1, SUB)}
            row, inv_row = over_sublanes(rows[m], k), over_sublanes(inv[m], k)
            for r in live:
                c = cols[r, k] * scale
                if r == m:
                    c = jnp.where(sub > k, c, 0.0)
                for j in range(k + 1, SUB):
                    cols[r, j] = cols[r, j] - c * ahead[j]
                rows[r] = rows[r] - c * row
                inv[r] = inv[r] - c * inv_row
        inv[m] = inv[m] * lax.rsqrt(pivots)
    return jnp.concatenate(inv, axis=0)


def factor_kernel(ps_ref, pf_ref, hi_ref, lo_ref, a_ref, w_ref):
    total = jnp.zeros((1, BLOCK), jnp.float32)
    for r in range(BLOCK // PANEL):
        at = slice(r * PANEL, (r + 1) * PANEL)
        inter = dot_nt(pf_ref[at, :], pf_ref[...])
        total = total + jnp.sum(jnp.abs(inter), axis=0, keepdims=True)
        kern = jnp.exp(dot_nt(ps_ref[at, :], ps_ref[...]) / ps_ref.shape[1] - 1.0)
        a_ref[at, :] = kern - inter
    shift = ridge_shift + jnp.max(total)
    row_ids = lax.broadcasted_iota(jnp.int32, (PANEL, BLOCK), 0)
    lane_ids = lax.broadcasted_iota(jnp.int32, (PANEL, BLOCK), 1)
    for r in range(BLOCK // PANEL):
        at = slice(r * PANEL, (r + 1) * PANEL)
        eye = lane_ids == row_ids + r * PANEL
        a_ref[at, :] = a_ref[at, :] + jnp.where(eye, shift, 0.0)
        w_ref[at, :] = jnp.where(eye, 1.0, 0.0)

    @pl.loop(0, BLOCK // PANEL)
    def _(j):
        start = pl.multiple_of(j * PANEL, PANEL)
        at = pl.ds(start, PANEL)
        inv = panel_inverse(a_ref[at, at])
        right = jnp.dot(inv, a_ref[at, :], precision=HIGHEST, preferred_element_type=jnp.float32)
        right = jnp.where(lane_ids >= start + PANEL, right, 0.0)
        done = jnp.dot(inv, w_ref[at, :], precision=HIGHEST, preferred_element_type=jnp.float32)
        w_ref[at, :] = done
        for r in range(1, BLOCK // PANEL):
            rows = slice(r * PANEL, (r + 1) * PANEL)

            @pl.when(j < r)
            def _():
                left = right[:, rows].T
                a_ref[rows, :] = a_ref[rows, :] - jnp.dot(
                    left, right, precision=HIGHEST, preferred_element_type=jnp.float32
                )
                w_ref[rows, :] = w_ref[rows, :] - jnp.dot(
                    left, done, precision=HIGHEST, preferred_element_type=jnp.float32
                )

    high = w_ref[...].astype(jnp.bfloat16)
    hi_ref[...] = high
    lo_ref[...] = (w_ref[...] - high.astype(jnp.float32)).astype(jnp.bfloat16)


def block_factor(pivot_scaled, pivot_factor):
    square = jax.ShapeDtypeStruct((BLOCK, BLOCK), jnp.bfloat16)
    return pl.pallas_call(
        factor_kernel,
        out_shape=(square, square),
        in_specs=[pl.BlockSpec(memory_space=pltpu.VMEM)] * 2,
        out_specs=[pl.BlockSpec(memory_space=pltpu.VMEM)] * 2,
        scratch_shapes=[pltpu.VMEM((BLOCK, BLOCK), jnp.float32)] * 2,
        name="block_factor",
    )(pivot_scaled, pivot_factor)


def columns_kernel(
    points_ref, factor_ref, targets_ref, ps_ref, pf_ref, hi_ref, lo_ref,
    new_ref, cross_ref, norm_ref, acc_ref, fsq_ref, nsq_ref,
):
    step = pl.program_id(0)
    held = factor_ref.shape[1]

    @pl.when(step == 0)
    def _():
        acc_ref[...] = jnp.zeros_like(acc_ref)
        fsq_ref[...] = jnp.zeros_like(fsq_ref)
        nsq_ref[...] = jnp.zeros_like(nsq_ref)

    scaled = normalize(points_ref[...])
    factor = factor_ref[...]
    down = jnp.exp(dot_nt(ps_ref[...], scaled) / scaled.shape[1] - 1.0) - dot_nt(
        pf_ref[...], factor
    )
    down_hi = down.astype(jnp.bfloat16)
    down_lo = (down - down_hi.astype(jnp.float32)).astype(jnp.bfloat16)
    half = BLOCK // 2
    for top, wide in ((0, half), (half, BLOCK)):
        at = slice(top, top + half)
        new_ref[at, :] = (
            dot_nn(hi_ref[at, :wide], down_hi[:wide])
            + dot_nn(hi_ref[at, :wide], down_lo[:wide])
            + dot_nn(lo_ref[at, :wide], down_hi[:wide])
        ).astype(jnp.bfloat16)
    new = new_ref[...]
    turned = targets_ref[...].T
    acc_ref[:, :held] += dot_nn(turned, factor)
    acc_ref[:, held:] += dot_nt(turned, new)
    wide_factor = factor.astype(jnp.float32)
    fsq_ref[...] += jnp.sum(
        (wide_factor * wide_factor).reshape(-1, SUB, held), axis=0
    )
    wide_new = new.astype(jnp.float32)
    squares = wide_new * wide_new
    nsq = nsq_ref[...]
    for t in range(new.shape[1] // 128):
        nsq = nsq + squares[:, t * 128 : (t + 1) * 128]
    nsq_ref[...] = nsq

    @pl.when(step == pl.num_programs(0) - 1)
    def _():
        held_norm = jnp.sum(fsq_ref[...], axis=0, keepdims=True)
        new_norm = jnp.sum(nsq_ref[...].T, axis=0, keepdims=True)
        norms = jnp.concatenate([held_norm, new_norm], axis=1)
        for t in range(norms.shape[1] // 128):
            lanes = slice(t * 128, (t + 1) * 128)
            norm_ref[t : t + 1, :] = norms[:, lanes]
            piece = acc_ref[:, lanes].astype(jnp.bfloat16)
            cross_ref[:, t * 8 : (t + 1) * 8] = piece.reshape(2, 8, 16, 128)


def columns_call(points, factor, targets, pivot_scaled, pivot_factor, inv_hi, inv_lo):
    pts, held = factor.shape
    features, wanted = points.shape[1], targets.shape[1]
    tiles = (held + BLOCK) // 128
    whole = lambda i: (0, 0)
    once = pl.Buffered(1)
    return pl.pallas_call(
        columns_kernel,
        grid=(pts // TILE_PTS,),
        out_shape=(
            jax.ShapeDtypeStruct((BLOCK, pts), jnp.bfloat16),
            jax.ShapeDtypeStruct((2, tiles * 8, 16, 128), jnp.bfloat16),
            jax.ShapeDtypeStruct((tiles, 128), jnp.float32),
        ),
        in_specs=[
            pl.BlockSpec((TILE_PTS, features), lambda i: (i, 0)),
            pl.BlockSpec((TILE_PTS, held), lambda i: (i, 0)),
            pl.BlockSpec((TILE_PTS, wanted), lambda i: (i, 0)),
            pl.BlockSpec((BLOCK, features), whole, pipeline_mode=once),
            pl.BlockSpec((BLOCK, held), whole, pipeline_mode=once),
            pl.BlockSpec((BLOCK, BLOCK), whole, pipeline_mode=once),
            pl.BlockSpec((BLOCK, BLOCK), whole, pipeline_mode=once),
        ],
        out_specs=[
            pl.BlockSpec((BLOCK, TILE_PTS), lambda i: (0, i)),
            pl.BlockSpec((2, tiles * 8, 16, 128), lambda i: (0, 0, 0, 0)),
            pl.BlockSpec((tiles, 128), whole),
        ],
        scratch_shapes=[
            pltpu.VMEM((wanted, held + BLOCK), jnp.float32),
            pltpu.VMEM((SUB, held), jnp.float32),
            pltpu.VMEM((BLOCK, 128), jnp.float32),
        ],
        name="new_columns",
    )(points, factor, targets, pivot_scaled, pivot_factor, inv_hi, inv_lo)


PARTS = (((0, 1, 2), 0, 64), ((1, 2, 0), 64, 48), ((2, 0, 1), 112, 48))


def place():
    row, col = lax.axis_index("row"), lax.axis_index("col")
    core = lax.rem(row, 2)
    coords = (lax.div(col, 4), lax.div(row, 2), lax.rem(col, 4))
    return core, coords


def device_at(core, coords, axis=0, offset=0):
    x, y, z = (
        lax.rem(c + offset, 4) if (a == axis and offset) else c for a, c in enumerate(coords)
    )
    return (y * 2 + core, x * 4 + z)


def enter(core, coords):
    barrier = pltpu.get_barrier_semaphore()
    peers = [device_at(1 - core, coords)]
    peers += [device_at(core, coords, a, o) for a in range(3) for o in range(1, 4)]
    for peer in peers:
        pl.semaphore_signal(barrier, inc=1, device_id=peer, device_id_type=MESH)
    pl.semaphore_wait(barrier, len(peers))


def sums_kernel(
    x_ref, n_ref, out_ref, got0, sum0, out0, norm_got0, norm_sum, norm_got, coef, got_last,
    a0, a1, a2, b0, b1, b2, c0, c1, c2, s1, s2, s3, t1, t2, t3, u1, u2, u3,
    send, recv,
):
    core, coords = place()
    partner = device_at(1 - core, coords)
    enter(core, coords)
    count = [0]
    sent = []

    def start(src, dst, device):
        k = count[0]
        count[0] += 1
        copy = pltpu.make_async_remote_copy(
            src_ref=src, dst_ref=dst, send_sem=send.at[k], recv_sem=recv.at[k],
            device_id=device, device_id_type=MESH,
        )
        copy.start()
        sent.append(copy)
        return copy

    def arrive(copies):
        for copy in copies:
            copy.wait_recv()

    wide = lambda v: v.astype(jnp.float32)
    narrow = lambda v: v.astype(jnp.bfloat16)

    arrive([
        start(x_ref.at[1 - core], got0, partner),
        start(n_ref, norm_got0, partner),
    ])
    sum0[...] = wide(x_ref[core]) + wide(got0[...])
    out0[...] = narrow(sum0[...])
    norm_sum[0] = n_ref[...] + norm_got0[...]

    got = ((a0, a1, a2), (b0, b1, b2), (c0, c1, c2))
    sums = ((s1, s2, s3), (t1, t2, t3))
    outs = (u1, u2, u3)

    copies, starts = [], []
    for p, (order, base, size) in enumerate(PARTS):
        here, quarter = coords[order[0]], size // 4
        for o in range(1, 4):
            there = lax.rem(here + o, 4)
            copies.append(
                start(
                    out0.at[pl.ds(base + there * quarter, quarter)],
                    got[0][p].at[o - 1],
                    device_at(core, coords, order[0], o),
                )
            )
        starts.append(base + here * quarter)
    for o in range(1, 4):
        copies.append(
            start(norm_sum.at[0], norm_got.at[0, o - 1], device_at(core, coords, 0, o))
        )
    arrive(copies)
    for p, (order, base, size) in enumerate(PARTS):
        quarter = size // 4
        value = sum0[pl.ds(starts[p], quarter)]
        for o in range(3):
            value = value + wide(got[0][p][o])
        sums[0][p][...] = value
        outs[p][...] = narrow(value)
    norm_sum[1] = norm_sum[0] + norm_got[0, 0] + norm_got[0, 1] + norm_got[0, 2]

    copies = []
    for p, (order, base, size) in enumerate(PARTS):
        here, piece = coords[order[1]], size // 16
        for o in range(1, 4):
            there = lax.rem(here + o, 4)
            copies.append(
                start(
                    outs[p].at[pl.ds(there * piece, piece)],
                    got[1][p].at[o - 1],
                    device_at(core, coords, order[1], o),
                )
            )
        starts[p] = starts[p] + here * piece
    for o in range(1, 4):
        copies.append(
            start(norm_sum.at[1], norm_got.at[1, o - 1], device_at(core, coords, 1, o))
        )
    arrive(copies)
    for p, (order, base, size) in enumerate(PARTS):
        here, piece = coords[order[1]], size // 16
        value = sums[0][p][pl.ds(here * piece, piece)]
        for o in range(3):
            value = value + wide(got[1][p][o])
        sums[1][p][0] = value
        coef[pl.ds(starts[p], piece)] = narrow(value)
    norm_sum[2] = norm_sum[1] + norm_got[1, 0] + norm_got[1, 1] + norm_got[1, 2]

    copies = []
    for p, (order, base, size) in enumerate(PARTS):
        piece = size // 16
        for o in range(1, 4):
            copies.append(
                start(
                    coef.at[pl.ds(starts[p], piece)],
                    got[2][p].at[o - 1],
                    device_at(core, coords, order[2], o),
                )
            )
    for o in range(1, 4):
        copies.append(
            start(norm_sum.at[2], norm_got.at[2, o - 1], device_at(core, coords, 2, o))
        )
    arrive(copies)
    for copy in copies:
        copy.wait_send()
    del sent[-len(copies):]
    norm_sum[3] = norm_sum[2] + norm_got[2, 0] + norm_got[2, 1] + norm_got[2, 2]
    for p, (order, base, size) in enumerate(PARTS):
        piece = size // 16
        value = sums[1][p][0]
        for o in range(3):
            value = value + wide(got[2][p][o])
        for i in range(piece):
            tile = lax.div(starts[p] + i, 8)
            norm = norm_sum[3, pl.ds(tile, 1), :]
            coef[starts[p] + i] = narrow(value[i] / (norm + damping))

    for stage, parts_of in ((1, 16), (0, 4)):
        copies = []
        for p, (order, base, size) in enumerate(PARTS):
            piece = size // parts_of
            if stage == 0:
                starts[p] = base + coords[order[0]] * piece
            block = coef.at[pl.ds(starts[p], piece)]
            for o in range(1, 4):
                copies.append(start(block, block, device_at(core, coords, order[stage], o)))
        arrive(copies)
    last = start(coef, got_last, partner)
    out_ref[core] = coef[...]
    last.wait_recv()
    out_ref[1 - core] = got_last[...]
    for copy in sent:
        copy.wait_send()


def sums_call(cross, norms):
    blocks, tiles = cross.shape[1], norms.shape[0]
    bf, f32, vmem = jnp.bfloat16, jnp.float32, pltpu.VMEM
    piece = lambda lead, n, kind: vmem((*lead, n, 16, 128), kind)
    sizes = [size for _, _, size in PARTS]
    scratch = [
        vmem((blocks, 16, 128), bf), vmem((blocks, 16, 128), f32), vmem((blocks, 16, 128), bf),
        vmem((tiles, 128), f32), vmem((4, tiles, 128), f32), vmem((3, 3, tiles, 128), f32),
        vmem((blocks, 16, 128), bf), vmem((blocks, 16, 128), bf),
    ]
    scratch += [piece((3,), s // 4, bf) for s in sizes]
    scratch += [piece((3,), s // 16, bf) for s in sizes]
    scratch += [piece((3,), s // 16, bf) for s in sizes]
    scratch += [piece((), s // 4, f32) for s in sizes]
    scratch += [piece((1,), s // 16, f32) for s in sizes]
    scratch += [piece((), s // 4, bf) for s in sizes]
    copies = 2 + 12 * 3 + 9 * 2 + 1
    scratch += [pltpu.SemaphoreType.DMA((copies,))] * 2
    return pl.pallas_call(
        sums_kernel,
        out_shape=jax.ShapeDtypeStruct(cross.shape, bf),
        in_specs=[pl.BlockSpec(memory_space=vmem)] * 2,
        out_specs=pl.BlockSpec(memory_space=vmem),
        scratch_shapes=scratch,
        compiler_params=pltpu.CompilerParams(collective_id=1, has_side_effects=True),
        name="sums",
    )(cross, norms)


def residual_kernel(factor_ref, new_ref, targets_ref, coef_ref, out_ref, turned_ref):
    held = factor_ref.shape[1]

    @pl.when(pl.program_id(0) == 0)
    def _():
        for t in range(turned_ref.shape[1] // 128):
            lanes = slice(t * 128, (t + 1) * 128)
            turned_ref[:, lanes] = coef_ref[:, t * 8 : (t + 1) * 8].reshape(-1, 128)

    fitted = dot_nt(factor_ref[...], turned_ref[:, :held])
    fitted = fitted + dot_nn(turned_ref[:, held:], new_ref[...]).T
    out_ref[...] = targets_ref[...].astype(jnp.float32) - fitted


def residual_call(factor, new, targets, coef):
    pts, held = factor.shape
    wanted = targets.shape[1]
    return pl.pallas_call(
        residual_kernel,
        grid=(pts // TILE_PTS,),
        out_shape=jax.ShapeDtypeStruct((pts, wanted), jnp.float32),
        in_specs=[
            pl.BlockSpec((TILE_PTS, held), lambda i: (i, 0)),
            pl.BlockSpec((BLOCK, TILE_PTS), lambda i: (0, i)),
            pl.BlockSpec((TILE_PTS, wanted), lambda i: (i, 0)),
            pl.BlockSpec(coef.shape, lambda i: (0, 0, 0, 0), pipeline_mode=pl.Buffered(1)),
        ],
        out_specs=pl.BlockSpec((TILE_PTS, wanted), lambda i: (i, 0)),
        scratch_shapes=[pltpu.VMEM((wanted, held + BLOCK), jnp.bfloat16)],
        name="residual",
    )(factor, new, targets, coef)


def on_device(points, factor, targets, pivot_slots, pivot_counts):
    local_slots = pivot_slots[0]
    slot_cap = pivot_slots.shape[1]
    own = jnp.concatenate(
        [
            normalize(jnp.take(points, local_slots, axis=0)),
            jnp.take(factor, local_slots, axis=0),
        ],
        axis=1,
    )
    inner = joined_along(sent_to_all(own, "col"), 0)
    padded = lax.all_gather(inner, "row", axis=0, tiled=True)
    owners, slot_index = compact_index(pivot_counts, BLOCK)
    pivots = jnp.take(padded, owners * slot_cap + slot_index, axis=0)
    pivot_scaled = pivots[:, : points.shape[1]]
    pivot_factor = pivots[:, points.shape[1] :]
    inv_hi, inv_lo = block_factor(pivot_scaled, pivot_factor)
    new_columns, cross, norms = columns_call(
        points, factor, targets, pivot_scaled, pivot_factor, inv_hi, inv_lo
    )
    coef = sums_call(cross, norms)
    residual_next = residual_call(factor, new_columns, targets, coef)
    return (new_columns, residual_next)


def solution(mesh):
    return jax.shard_map(
        on_device,
        mesh=mesh,
        in_specs=(
            P(("row", "col"), None),
            P(("row", "col"), None),
            P(("row", "col"), None),
            P(("row", "col"), None),
            P(),
        ),
        out_specs=(P(None, ("row", "col")), P(("row", "col"), None)),
        check_vma=False,
    )
```

time: 450 us -> 181 us (0.40)
  other arithmetic: 137 us -> 2.7 us
  Pallas kernels: 0 us -> 89.4 us
  waiting for transfers between devices: 109 us -> 35.7 us
  blocking collectives: 85.6 us -> 20 us
  matrix products: 51.6 us -> 0 us
  local copies, waits for them, and re-layouts: 44.5 us -> 18.5 us
    another operation x19 -> x2, other arithmetic: 120 us -> 0.27 us  [the longest x14 79 us: block_factor(): return jnp.linalg.cholesky(ridged)]
    pallas_call x0 -> x4, Pallas kernels: none -> 89.4 us  [the longest x1 34.5 us: sums_call(): pl.pallas_call(sums_kernel, out_shape=jax.ShapeDtypeStruct(cross.shape, b...]
    psum x1 -> x0, waiting for transfers between devices: 80.7 us -> none  [on_device(): cross_whole, norm_whole = lax.psum((cross_terms, col_norms), ('row', 'col'))]
    psum x1 -> x0, blocking collectives: 65.6 us -> none  [on_device(): cross_whole, norm_whole = lax.psum((cross_terms, col_norms), ('row', 'col'))]
    dot_general x8 -> x0, matrix products: 34.9 us -> none  [the longest x1 9.73 us: on_device(): lax.dot_general(pivot_factor, factor, (((1,), (1,)), ((), ())), preferred...]
    another operation x13 -> x0, matrix products: 16.7 us -> none  [the longest x7 11.3 us: on_device(): lax.linalg.triangular_solve(lower_factor, downdated, left_side=True, lowe...]
    another operation x18 -> x1, local copies, waits for them, and re-layouts: 14.4 us -> 0.11 us
    all_gather x1, waiting for transfers between devices: 27.9 us -> 35.6 us  [on_device(): padded = lax.all_gather(inner, 'row', axis=0, tiled=True)]
  transfers between devices with their start and end apart: 2 -> 1, of which waited for: 2 -> 1; matrix products, arithmetic and copies ran while one was open for 3% -> 0% of each run, Pallas kernels for 0% -> 0%
where the time goes in v1:
time: 181 us; the launch traced here: 180 us
  Pallas kernels  89.4 us (49%)
  waiting for transfers between devices  35.7 us (20%)
  blocking collectives  20 us (11%)
  local copies, waits for them, and re-layouts  18.5 us (10%)
  between operations  14.1 us (8%)
  other arithmetic  2.7 us (1%)
    all_gather x1, waiting for transfers between devices, on_device(): padded = lax.all_gather(inner, 'row', axis=0, tiled=True)  35.6 us
    pallas_call x1, Pallas kernels, sums_call(): pl.pallas_call(sums_kernel, out_shape=jax.ShapeDtypeStruct(cross.shape, b...  34.5 us
    pallas_call x1, Pallas kernels, block_factor(): pl.pallas_call(factor_kernel, out_shape=(square, square), in_specs=[pl.Bl...  28.7 us
    all_to_all x1, blocking collectives, sent_to_all(): return lax.all_to_all(copies, axis, split_axis=0, concat_axis=0, tiled=True)  20 us
    pallas_call x1, Pallas kernels, columns_call(): pl.pallas_call(columns_kernel, grid=(pts // TILE_PTS,), out_shape=(jax.Sh...  17.9 us
    gather x1, local copies, waits for them, and re-layouts, on_device(): pivots = jnp.take(padded, owners * slot_cap + slot_index, axis=0)  8.37 us
    pallas_call x1, Pallas kernels, residual_call(): pl.pallas_call(residual_kernel, grid=(pts // TILE_PTS,), out_shape=jax.Sh...  8.25 us
    gather x1, local copies, waits for them, and re-layouts, on_device(): jnp.take(factor, local_slots, axis=0)  5.07 us
  transfers between devices with their start and end apart: 1, of which 1 were waited for; matrix products, arithmetic and copies ran while one was open for 0% of the time, Pallas kernels for 0%

profile of v1, /device:TPU:1, one launch (start us, length us, event | category | flops | bytes accessed | tf_op | source)
XLA Modules:
  0.0 180.5 jit_solution(18049430087299421802)
XLA Ops:
  7.2 0.0 copy-start
  7.2 0.0 all-gather.2.cloned.1.call-start
  7.2 0.7 compare_and_fusion
  7.9 0.7 fusion.2
  8.6 2.4 %gather_fusion = bf16[8,512]{1,0:T(8,128)(2,1)S(1)} fusion(bf16[2048,512]{1,0:T(8,128)(2,1)} %points_ref.1, s32[1024]{0:T(1024)S(1)} %pad_clamp_fusion.1), kind=kCustom, calls=%fused_computation | custom fusion | bytes 16416 | tf_op jit(solution)/shard_map/jit(_take)/gather | solution.py:483
  11.0 0.2 fusion
  11.2 0.1 fusion.1
  11.3 5.1 %gather_fusion.1 = bf16[8,2048]{1,0:T(8,128)(2,1)S(1)} fusion(bf16[2048,2048]{1,0:T(8,128)(2,1)} %factor_ref.3, s32[1024]{0:T(1024)S(1)} %pad_clamp_fusion.1), kind=kCustom, calls=%fused_computation.1 | custom fusion | bytes 65568 | tf_op jit(solution)/shard_map/jit(_take)/gather | solution.py:484
  16.3 0.1 broadcast_select_fusion.1
  16.5 20.0 %all_to_all.5 = bf16[16,8,2560]{2,1,0:T(8,128)(2,1)} all-to-all(bf16[16,8,2560]{2,1,0:T(8,128)(2,1)S(1)} %broadcast_in_dim.44), channel_id=1, replica_groups=mesh['row'=8,'col'=16] {'col'}, dimensions={0} | all-to-all | bytes 1310720 | tf_op jit(solution)/shard_map/all_to_all | solution.py:30
  36.5 0.0 all-gather.2.cloned.1.call-update
  36.5 0.0 copy-done
  36.5 0.1 copy.9
  36.6 0.2 reduce-window.8
  36.8 0.1 reduce
  36.9 0.2 convert_reduce_fusion
  37.1 0.2 select_reduce_fusion
  37.4 35.6 %all-gather.2.cloned.1.call-done = bf16[1024,2560]{1,0:T(8,128)(2,1)} async-done(((bf16[128,2560]{1,0:T(8,128)(2,1)}), bf16[1024,2560]{1,0:T(8,128)(2,1)}) %all-gather.2.cloned.1.call-update) | async-done | bytes 5242896 | tf_op jit(solution)/shard_map/all_gather | solution.py:489
  73.0 8.4 %gather_fusion.2 = bf16[512,2560]{1,0:T(8,128)(2,1)S(1)} fusion(bf16[1024,2560]{1,0:T(8,128)(2,1)} %all-gather.2.cloned.1.call-done, s32[1024]{0:T(1024)S(1)} %pad_clamp_fusion), kind=kCustom, calls=%fused_computation.2 | custom fusion | bytes 5244928 | tf_op jit(solution)/shard_map/jit(_take)/gather | solution.py:491
  81.4 0.3 broadcast_select_fusion
  81.7 0.9 slice.14.ps_ref
  82.6 1.6 slice.15.pf_ref
  84.2 28.7 %block_factor.1 = (bf16[512,512]{1,0:T(8,128)(2,1)}, bf16[512,512]{1,0:T(8,128)(2,1)}) custom-call(bf16[512,512]{1,0:T(8,128)(2,1)} %slice.14.ps_ref, bf16[512,2048]{1,0:T(8,128)(2,1)} %slice.15.pf_ref), custom_call_target="tpu_custom_call" | custom-call | tf_op jit(solution)/shard_map/block_factor/pallas_call | solution.py:145
  112.9 17.9 %new_columns.1 = (bf16[512,2048]{1,0:T(8,128)(2,1)}, bf16[2,160,16,128]{3,2,1,0:T(8,128)(2,1)}, f32[20,128]{1,0:T(8,128)}) custom-call(bf16[2048,512]{1,0:T(8,128)(2,1)} %points_ref.1, bf16[2048,2048]{1,0:T(8,128)(2,1)} %factor_ref.3, bf16[2048,256]{1,0:T(8,128)(2,1)} %targets_ref.3, bf16[512,512]{1,0:T(8,128)(2,1)} %slice.14.ps_ref, ...), custom_call_target="tpu_custom_call" | custom-call | tf_op jit(solution)/shard_map/new_columns/pallas_call | solution.py:216
  130.9 34.5 %sums.1.coef_ref = bf16[2,160,16,128]{3,2,1,0:T(8,128)(2,1)} custom-call(bf16[2,160,16,128]{3,2,1,0:T(8,128)(2,1)} %get-tuple-element.10.x_ref, f32[20,128]{1,0:T(8,128)} %get-tuple-element.11.n_ref), custom_call_target="tpu_custom_call" | custom-call | tf_op jit(solution)/shard_map/sums/pallas_call | solution.py:434
  165.4 8.2 %residual.1 = f32[2048,256]{1,0:T(8,128)} custom-call(bf16[2048,2048]{1,0:T(8,128)(2,1)} %factor_ref.3, bf16[512,2048]{1,0:T(8,128)(2,1)} %get-tuple-element.5.new_ref, bf16[2048,256]{1,0:T(8,128)(2,1)} %targets_ref.3, bf16[2,160,16,128]{3,2,1,0:T(8,128)(2,1)} %sums.1.coef_ref), custom_call_target="tpu_custom_call" | custom-call | tf_op jit(solution)/shard_map/residual/pallas_call | solution.py:462
  (9 shorter events, 0.1 us)
Async XLA Ops:
  7.2 29.3 %copy-start = (s32[128]{0:T(128)S(1)}, s32[128]{0:T(128)}, u32[]{:S(2)}) copy-start(s32[128]{0:T(128)} %param.9) | copy-start | bytes 1540
  7.2 65.8 %all-gather.2.cloned.1.call-start = ((), (), s32[]{:S(2)}) async-start(), calls=%async_computation.1 | async-start | bytes 5898240 | tf_op jit(solution)/shard_map/all_gather | solution.py:489
Sparse Core Ops, SparseCore 0:
  36.6 36.3 all-gather.1

commit v2 on v1

--- a/solution.py
+++ b/solution.py
@@ -19,35 +19,17 @@
 epsilon = 1e-06
 
 
-def joined_along(blocks, dim):
-    shape = list(blocks.shape[1:])
-    shape[dim] *= blocks.shape[0]
-    return jnp.moveaxis(blocks, 0, dim).reshape(shape)
-
-
-def sent_to_all(shard, axis):
-    copies = jnp.broadcast_to(shard, (lax.axis_size(axis), *shard.shape))
-    return lax.all_to_all(copies, axis, split_axis=0, concat_axis=0, tiled=True)
-
-
 def normalize(points):
     values = points.astype(jnp.float32)
     factor_scale = lax.rsqrt(jnp.mean(values * values, axis=1, keepdims=True) + epsilon)
     return (values * factor_scale).astype(jnp.bfloat16)
 
 
-def compact_index(pivot_counts, block_size):
-    owners_count = pivot_counts.shape[0]
-    run_ends = jnp.cumsum(pivot_counts).astype(jnp.int32)
-    run_starts = (run_ends - pivot_counts).astype(jnp.int32)
-    position = jnp.arange(block_size, dtype=jnp.int32)
-    owners = jnp.sum((position[:, None] >= run_ends[None, :]).astype(jnp.int32), axis=1)
-    owners = owners.astype(jnp.int32)
-    onehot = (owners[:, None] == jnp.arange(owners_count, dtype=jnp.int32)[None, :]).astype(
-        jnp.int32
-    )
-    first_row = jnp.sum(onehot * run_starts[None, :], axis=1)
-    return (owners, position - first_row)
+def padded_positions(pivot_counts, slot_cap):
+    starts = jnp.cumsum(pivot_counts) - pivot_counts
+    slot = jnp.arange(slot_cap, dtype=jnp.int32)[None, :]
+    place_of = jnp.where(slot < pivot_counts[:, None], starts[:, None] + slot, -1)
+    return place_of.astype(jnp.int32).reshape(1, -1)
 
 
 def dot_nt(a, b):
@@ -56,6 +38,186 @@
 
 def dot_nn(a, b):
     return jnp.dot(a, b, preferred_element_type=jnp.float32)
+
+
+PARTS = (((0, 1, 2), 0, 64), ((1, 2, 0), 64, 48), ((2, 0, 1), 112, 48))
+
+
+def place():
+    row, col = lax.axis_index("row"), lax.axis_index("col")
+    core = lax.rem(row, 2)
+    coords = (lax.div(col, 4), lax.div(row, 2), lax.rem(col, 4))
+    return core, coords
+
+
+def device_at(core, coords, axis=0, offset=0):
+    x, y, z = (
+        lax.rem(c + offset, 4) if (a == axis and offset) else c for a, c in enumerate(coords)
+    )
+    return (y * 2 + core, x * 4 + z)
+
+
+def enter(core, coords):
+    barrier = pltpu.get_barrier_semaphore()
+    peers = [device_at(1 - core, coords)]
+    peers += [device_at(core, coords, a, o) for a in range(3) for o in range(1, 4)]
+    for peer in peers:
+        pl.semaphore_signal(barrier, inc=1, device_id=peer, device_id_type=MESH)
+    pl.semaphore_wait(barrier, len(peers))
+
+
+def rows_kernel(slots_ref, points_ref, factor_ref, out_ref, pbuf, fbuf, psem, fsem):
+    cap = pbuf.shape[0]
+    copies = []
+    for s in range(cap):
+        base = pl.multiple_of(lax.div(slots_ref[0, s], SUB) * SUB, SUB)
+        for src, buf, sem in ((points_ref, pbuf, psem), (factor_ref, fbuf, fsem)):
+            copy = pltpu.make_async_copy(src.at[pl.ds(base, SUB), :], buf.at[s], sem.at[s])
+            copy.start()
+            copies.append(copy)
+    for copy in copies:
+        copy.wait()
+
+    def picked(buf):
+        sub = lax.broadcasted_iota(jnp.int32, buf.shape[1:], 0)
+        out = jnp.zeros(buf.shape[1:], jnp.float32)
+        for s in range(cap):
+            offset = lax.rem(slots_ref[0, s], SUB)
+            row = jnp.sum(
+                jnp.where(sub == offset, buf[s].astype(jnp.float32), 0.0), axis=0, keepdims=True
+            )
+            out = jnp.where(sub == s, row, out)
+        return out
+
+    both = (normalize(picked(pbuf)), picked(fbuf).astype(jnp.bfloat16))
+    t = 0
+    for rows in both:
+        for k in range(rows.shape[1] // 128):
+            out_ref[t] = rows[:, k * 128 : (k + 1) * 128]
+            t += 1
+
+
+def rows_call(pivot_slots, points, factor):
+    cap = pivot_slots.shape[1]
+    features, held = points.shape[1], factor.shape[1]
+    return pl.pallas_call(
+        rows_kernel,
+        out_shape=jax.ShapeDtypeStruct(((features + held) // 128, cap, 128), jnp.bfloat16),
+        in_specs=[
+            pl.BlockSpec(memory_space=pltpu.SMEM),
+            pl.BlockSpec(memory_space=pl.ANY),
+            pl.BlockSpec(memory_space=pl.ANY),
+        ],
+        out_specs=pl.BlockSpec(memory_space=pltpu.VMEM),
+        scratch_shapes=[
+            pltpu.VMEM((cap, SUB, features), jnp.bfloat16),
+            pltpu.VMEM((cap, SUB, held), jnp.bfloat16),
+            pltpu.SemaphoreType.DMA((cap,)),
+            pltpu.SemaphoreType.DMA((cap,)),
+        ],
+        name="pivot_rows",
+    )(pivot_slots, points, factor)
+
+
+SPANS = ((0, 4, 7), (7, 11, 14), (14, 17, 20))
+
+
+def gather_kernel(own_ref, out_ref, send, recv):
+    core, coords = place()
+    partner = device_at(1 - core, coords)
+    enter(core, coords)
+    count = [0]
+    sent = []
+
+    def start(src, dst, device):
+        k = count[0]
+        count[0] += 1
+        copy = pltpu.make_async_remote_copy(
+            src_ref=src, dst_ref=dst, send_sem=send.at[k], recv_sem=recv.at[k],
+            device_id=device, device_id_type=MESH,
+        )
+        copy.start()
+        sent.append(copy)
+        return copy
+
+    def region(low, high, whole=(), axis=None, at=None):
+        x, y, z = (
+            slice(None) if a in whole else (at if a == axis else c)
+            for a, c in enumerate(coords)
+        )
+        return out_ref.at[y, core, x, z, low:high]
+
+    def push(block, device):
+        return start(block, block, device)
+
+    first = []
+    for (order, _, _), (low, _, high) in zip(PARTS, SPANS):
+        first.append([
+            start(own_ref.at[low:high], region(low, high), device_at(core, coords, order[0], o))
+            for o in (2, 1, 3)
+        ])
+    x, y, z = coords
+    out_ref[y, core, x, z] = own_ref[...]
+    second = []
+    for p, ((order, _, _), (low, _, high)) in enumerate(zip(PARTS, SPANS)):
+        for copy in first[p]:
+            copy.wait_recv()
+        block = region(low, high, order[:1])
+        second.append([
+            push(block, device_at(core, coords, order[1], o)) for o in (2, 1, 3)
+        ])
+    third, across = [], []
+    for p, ((order, _, _), (low, mid, high)) in enumerate(zip(PARTS, SPANS)):
+        for copy in second[p]:
+            copy.wait_recv()
+        left, right = (device_at(core, coords, order[2], o) for o in (3, 1))
+        halves = [region(a, b, order[:2]) for a, b in ((low, mid), (mid, high))]
+        right_low = push(halves[0], right)
+        left_high = push(halves[1], left)
+        right_high = push(halves[1], right)
+        left_low = push(halves[0], left)
+        third.append((right_low, left_high, right_high, left_low))
+        across.append(push(region(low, high, order[:2]), partner))
+    relays = []
+    for p, ((order, _, _), (low, mid, high)) in enumerate(zip(PARTS, SPANS)):
+        axis = order[2]
+        before, after = (lax.rem(coords[axis] + o, 4) for o in (3, 1))
+        left, right = (device_at(core, coords, axis, o) for o in (3, 1))
+        third[p][0].wait_recv()
+        one = push(region(low, mid, order[:2], axis, before), right)
+        third[p][1].wait_recv()
+        relays.append((one, push(region(mid, high, order[:2], axis, after), left)))
+    for p, ((order, _, _), (low, mid, high)) in enumerate(zip(PARTS, SPANS)):
+        axis = order[2]
+        before, after = (lax.rem(coords[axis] + o, 4) for o in (3, 1))
+        third[p][2].wait_recv()
+        across.append(push(region(low, high, order[:2], axis, before), partner))
+        third[p][3].wait_recv()
+        across.append(push(region(low, high, order[:2], axis, after), partner))
+    for p, ((order, _, _), (low, mid, high)) in enumerate(zip(PARTS, SPANS)):
+        axis = order[2]
+        opposite = lax.rem(coords[axis] + 2, 4)
+        for copy, (a, b) in zip(relays[p], ((low, mid), (mid, high))):
+            copy.wait_recv()
+            across.append(push(region(a, b, order[:2], axis, opposite), partner))
+    for copy in across:
+        copy.wait_recv()
+    for copy in sent:
+        copy.wait_send()
+
+
+def gather_call(own):
+    copies = 9 + 9 + 12 + 3 + 6 + 6 + 6
+    out = pl.pallas_call(
+        gather_kernel,
+        out_shape=jax.ShapeDtypeStruct((4, 2, 4, 4, *own.shape), own.dtype),
+        in_specs=[pl.BlockSpec(memory_space=pltpu.VMEM)],
+        out_specs=pl.BlockSpec(memory_space=pltpu.VMEM),
+        scratch_shapes=[pltpu.SemaphoreType.DMA((copies,))] * 2,
+        compiler_params=pltpu.CompilerParams(collective_id=2, has_side_effects=True),
+        name="gather_rows",
+    )(own)
+    return out.reshape(128, *own.shape)
 
 
 def panel_inverse(block):
@@ -96,7 +258,22 @@
     return jnp.concatenate(inv, axis=0)
 
 
-def factor_kernel(ps_ref, pf_ref, hi_ref, lo_ref, a_ref, w_ref):
+def factor_kernel(pad_ref, pos_ref, ps_ref, pf_ref, hi_ref, lo_ref, a_ref, w_ref, sel_ref):
+    padded = pos_ref.shape[1]
+    sel_ref[...] = jnp.where(
+        lax.broadcasted_iota(jnp.int32, (BLOCK, padded), 0) == pos_ref[...], 1.0, 0.0
+    ).astype(jnp.bfloat16)
+    ahead = ps_ref.shape[1] // 128
+    for t in range(0, pad_ref.shape[1], 2):
+        pair = [
+            pad_ref[:, k].astype(jnp.float32).reshape(padded, 128).astype(jnp.bfloat16)
+            for k in (t, t + 1)
+        ]
+        rows = dot_nn(sel_ref[...], jnp.concatenate(pair, axis=1)).astype(jnp.bfloat16)
+        if t < ahead:
+            ps_ref[:, t * 128 : (t + 2) * 128] = rows
+        else:
+            pf_ref[:, (t - ahead) * 128 : (t - ahead + 2) * 128] = rows
     total = jnp.zeros((1, BLOCK), jnp.float32)
     for r in range(BLOCK // PANEL):
         at = slice(r * PANEL, (r + 1) * PANEL)
@@ -140,16 +317,23 @@
     lo_ref[...] = (w_ref[...] - high.astype(jnp.float32)).astype(jnp.bfloat16)
 
 
-def block_factor(pivot_scaled, pivot_factor):
-    square = jax.ShapeDtypeStruct((BLOCK, BLOCK), jnp.bfloat16)
+def block_factor(padded, positions, features):
+    held = padded.shape[1] * 128 - features
+    bf = jnp.bfloat16
     return pl.pallas_call(
         factor_kernel,
-        out_shape=(square, square),
+        out_shape=(
+            jax.ShapeDtypeStruct((BLOCK, features), bf),
+            jax.ShapeDtypeStruct((BLOCK, held), bf),
+            jax.ShapeDtypeStruct((BLOCK, BLOCK), bf),
+            jax.ShapeDtypeStruct((BLOCK, BLOCK), bf),
+        ),
         in_specs=[pl.BlockSpec(memory_space=pltpu.VMEM)] * 2,
-        out_specs=[pl.BlockSpec(memory_space=pltpu.VMEM)] * 2,
-        scratch_shapes=[pltpu.VMEM((BLOCK, BLOCK), jnp.float32)] * 2,
+        out_specs=[pl.BlockSpec(memory_space=pltpu.VMEM)] * 4,
+        scratch_shapes=[pltpu.VMEM((BLOCK, BLOCK), jnp.float32)] * 2
+        + [pltpu.VMEM((BLOCK, positions.shape[1]), bf)],
         name="block_factor",
-    )(pivot_scaled, pivot_factor)
+    )(padded, positions)
 
 
 def columns_kernel(
@@ -244,32 +428,6 @@
     )(points, factor, targets, pivot_scaled, pivot_factor, inv_hi, inv_lo)
 
 
-PARTS = (((0, 1, 2), 0, 64), ((1, 2, 0), 64, 48), ((2, 0, 1), 112, 48))
-
-
-def place():
-    row, col = lax.axis_index("row"), lax.axis_index("col")
-    core = lax.rem(row, 2)
-    coords = (lax.div(col, 4), lax.div(row, 2), lax.rem(col, 4))
-    return core, coords
-
-
-def device_at(core, coords, axis=0, offset=0):
-    x, y, z = (
-        lax.rem(c + offset, 4) if (a == axis and offset) else c for a, c in enumerate(coords)
-    )
-    return (y * 2 + core, x * 4 + z)
-
-
-def enter(core, coords):
-    barrier = pltpu.get_barrier_semaphore()
-    peers = [device_at(1 - core, coords)]
-    peers += [device_at(core, coords, a, o) for a in range(3) for o in range(1, 4)]
-    for peer in peers:
-        pl.semaphore_signal(barrier, inc=1, device_id=peer, device_id_type=MESH)
-    pl.semaphore_wait(barrier, len(peers))
-
-
 def sums_kernel(
     x_ref, n_ref, out_ref, got0, sum0, out0, norm_got0, norm_sum, norm_got, coef, got_last,
     a0, a1, a2, b0, b1, b2, c0, c1, c2, s1, s2, s3, t1, t2, t3, u1, u2, u3,
@@ -476,22 +634,12 @@
 
 
 def on_device(points, factor, targets, pivot_slots, pivot_counts):
-    local_slots = pivot_slots[0]
-    slot_cap = pivot_slots.shape[1]
-    own = jnp.concatenate(
-        [
-            normalize(jnp.take(points, local_slots, axis=0)),
-            jnp.take(factor, local_slots, axis=0),
-        ],
-        axis=1,
+    own = rows_call(pivot_slots, points, factor)
+    padded = gather_call(own)
+    positions = padded_positions(pivot_counts, pivot_slots.shape[1])
+    pivot_scaled, pivot_factor, inv_hi, inv_lo = block_factor(
+        padded, positions, points.shape[1]
     )
-    inner = joined_along(sent_to_all(own, "col"), 0)
-    padded = lax.all_gather(inner, "row", axis=0, tiled=True)
-    owners, slot_index = compact_index(pivot_counts, BLOCK)
-    pivots = jnp.take(padded, owners * slot_cap + slot_index, axis=0)
-    pivot_scaled = pivots[:, : points.shape[1]]
-    pivot_factor = pivots[:, points.shape[1] :]
-    inv_hi, inv_lo = block_factor(pivot_scaled, pivot_factor)
     new_columns, cross, norms = columns_call(
         points, factor, targets, pivot_scaled, pivot_factor, inv_hi, inv_lo
     )

time: 181 us -> 128 us (0.71)
  waiting for transfers between devices: 35.7 us -> 0 us
  Pallas kernels: 89.4 us -> 125 us
  blocking collectives: 20 us -> 0 us
  local copies, waits for them, and re-layouts: 18.5 us -> 0.81 us
  between operations: 14.1 us -> 0.7 us
  other arithmetic: 2.7 us -> 0.38 us
    pallas_call x1 -> x3, Pallas kernels: 28.7 us -> 67.6 us  [the longest x1 33.2 us: block_factor(): pl.pallas_call(factor_kernel, out_shape=(jax.ShapeDtypeStruct((BLOCK, fea...]
    all_gather x1 -> x0, waiting for transfers between devices: 35.6 us -> none  [on_device(): padded = lax.all_gather(inner, 'row', axis=0, tiled=True)]
    all_to_all x1 -> x0, blocking collectives: 20 us -> none  [sent_to_all(): return lax.all_to_all(copies, axis, split_axis=0, concat_axis=0, tiled=True)]
    gather x3 -> x0, local copies, waits for them, and re-layouts: 15.9 us -> none  [the longest x1 8.37 us: on_device(): pivots = jnp.take(padded, owners * slot_cap + slot_index, axis=0)]
    pallas_call x1, Pallas kernels: 34.5 us -> 31.7 us  [sums_call(): pl.pallas_call(sums_kernel, out_shape=jax.ShapeDtypeStruct(cross.shape, b...]
    slice x2 -> x0, local copies, waits for them, and re-layouts: 2.49 us -> none  [the longest x1 1.63 us: on_device(): pivot_factor = pivots[:, points.shape[1]:]]
  transfers between devices with their start and end apart: 1 -> 0, of which waited for: 1 -> 0; matrix products, arithmetic and copies ran while one was open for 0% -> 0% of each run, Pallas kernels for 0% -> 0%
where the time goes in v2:
time: 128 us; the launch traced here: 127 us
  Pallas kernels  125 us (98%)
    pallas_call x1, Pallas kernels, block_factor(): pl.pallas_call(factor_kernel, out_shape=(jax.ShapeDtypeStruct((BLOCK, fea...  33.2 us
    pallas_call x1, Pallas kernels, sums_call(): pl.pallas_call(sums_kernel, out_shape=jax.ShapeDtypeStruct(cross.shape, b...  31.7 us
    pallas_call x1, Pallas kernels, gather_call(): pl.pallas_call(gather_kernel, out_shape=jax.ShapeDtypeStruct((4, 2, 4, 4,...  31.6 us
    pallas_call x1, Pallas kernels, columns_call(): pl.pallas_call(columns_kernel, grid=(pts // TILE_PTS,), out_shape=(jax.Sh...  17.8 us
    pallas_call x1, Pallas kernels, residual_call(): pl.pallas_call(residual_kernel, grid=(pts // TILE_PTS,), out_shape=jax.Sh...  8.25 us
    pallas_call x1, Pallas kernels, rows_call(): pl.pallas_call(rows_kernel, out_shape=jax.ShapeDtypeStruct(((features + h...  2.73 us

profile of v2, /device:TPU:1, one launch (start us, length us, event | category | flops | bytes accessed | tf_op | source)
XLA Modules:
  0.0 127.2 jit_solution(16177900087609502832)
XLA Ops:
  0.6 0.0 copy-start
  0.6 2.7 %pivot_rows.1.own_ref = bf16[20,8,128]{2,1,0:T(8,128)(2,1)} custom-call(s32[1,8]{1,0:T(1,128)} %slots_ref.1, bf16[2048,512]{1,0:T(8,128)(2,1)} %points_ref.3, bf16[2048,2048]{1,0:T(8,128)(2,1)} %factor_ref.5), custom_call_target="tpu_custom_call" | custom-call | tf_op jit(solution)/shard_map/pivot_rows/pallas_call | solution.py:103
  3.4 0.0 copy-done
  3.4 0.1 copy.8
  3.5 0.2 reduce-window.9
  3.7 0.1 reduce
  3.8 0.1 add_select_fusion
  3.9 0.7 select_n.15.pos_ref
  4.6 31.6 %gather_rows.1 = bf16[4,2,4,4,20,8,128]{6,5,4,3,2,1,0:T(8,128)(2,1)} custom-call(bf16[20,8,128]{2,1,0:T(8,128)(2,1)} %pivot_rows.1.own_ref), custom_call_target="tpu_custom_call" | custom-call | tf_op jit(solution)/shard_map/gather_rows/pallas_call | solution.py:211
  36.3 33.2 %block_factor.1 = (bf16[512,512]{1,0:T(8,128)(2,1)}, bf16[512,2048]{1,0:T(8,128)(2,1)}, bf16[512,512]{1,0:T(8,128)(2,1)}, bf16[512,512]{1,0:T(8,128)(2,1)}) custom-call(bf16[128,20,8,128]{3,2,1,0:T(8,128)(2,1)} %bitcast.2, s32[1,1024]{1,0:T(1,128)} %select_n.15.pos_ref), custom_call_target="tpu_custom_call" | custom-call | tf_op jit(solution)/shard_map/block_factor/pallas_call | solution.py:323
  69.4 17.8 %new_columns.1 = (bf16[512,2048]{1,0:T(8,128)(2,1)}, bf16[2,160,16,128]{3,2,1,0:T(8,128)(2,1)}, f32[20,128]{1,0:T(8,128)}) custom-call(bf16[2048,512]{1,0:T(8,128)(2,1)} %points_ref.3, bf16[2048,2048]{1,0:T(8,128)(2,1)} %factor_ref.5, bf16[2048,256]{1,0:T(8,128)(2,1)} %targets_ref.3, bf16[512,512]{1,0:T(8,128)(2,1)} %get-tuple-element.9.ps_ref, ...), custom_call_target="tpu_custom_call" | custom-call | tf_op jit(solution)/shard_map/new_columns/pallas_call | solution.py:400
  87.2 31.7 %sums.1.coef_ref = bf16[2,160,16,128]{3,2,1,0:T(8,128)(2,1)} custom-call(bf16[2,160,16,128]{3,2,1,0:T(8,128)(2,1)} %get-tuple-element.14.x_ref, f32[20,128]{1,0:T(8,128)} %get-tuple-element.15.n_ref), custom_call_target="tpu_custom_call" | custom-call | tf_op jit(solution)/shard_map/sums/pallas_call | solution.py:592
  119.0 8.2 %residual.1 = f32[2048,256]{1,0:T(8,128)} custom-call(bf16[2048,2048]{1,0:T(8,128)(2,1)} %factor_ref.5, bf16[512,2048]{1,0:T(8,128)(2,1)} %get-tuple-element.7.new_ref, bf16[2048,256]{1,0:T(8,128)(2,1)} %targets_ref.3, bf16[2,160,16,128]{3,2,1,0:T(8,128)(2,1)} %sums.1.coef_ref), custom_call_target="tpu_custom_call" | custom-call | tf_op jit(solution)/shard_map/residual/pallas_call | solution.py:620
  (1 shorter events, 0.0 us)
Async XLA Ops:
  0.6 2.7 %copy-start = (s32[128]{0:T(128)S(1)}, s32[128]{0:T(128)}, u32[]{:S(2)}) copy-start(s32[128]{0:T(128)} %param.9) | copy-start | bytes 1540

commit v3 on v2

--- a/solution.py
+++ b/solution.py
@@ -38,6 +38,15 @@
 
 def dot_nn(a, b):
     return jnp.dot(a, b, preferred_element_type=jnp.float32)
+
+
+def put_blocks(acc, norms, cross_ref, norm_ref):
+    for t in range(norms.shape[1] // 128):
+        lanes = slice(t * 128, (t + 1) * 128)
+        norm_ref[t : t + 1, :] = norms[:, lanes]
+        cross_ref[:, t * 8 : (t + 1) * 8] = (
+            acc[:, lanes].astype(jnp.bfloat16).reshape(2, 8, 16, 128)
+        )
 
 
 PARTS = (((0, 1, 2), 0, 64), ((1, 2, 0), 64, 48), ((2, 0, 1), 112, 48))
@@ -122,7 +131,25 @@
 SPANS = ((0, 4, 7), (7, 11, 14), (14, 17, 20))
 
 
-def gather_kernel(own_ref, out_ref, send, recv):
+def gather_kernel(
+    own_ref, targets_ref, factor_ref, out_ref, cross_ref, norm_ref, fbuf, acc_ref, send, recv, fsem
+):
+    chunks = fbuf.shape[0]
+    loads = []
+    for i in range(chunks):
+        at = pl.ds(i * TILE_PTS, TILE_PTS)
+        load = pltpu.make_async_copy(factor_ref.at[at, :], fbuf.at[i], fsem.at[i])
+        load.start()
+        loads.append(load)
+    squares = [jnp.zeros((SUB, fbuf.shape[2]), jnp.float32)]
+
+    def add_chunk(i):
+        loads[i].wait()
+        value = dot_nn(targets_ref[i * TILE_PTS : (i + 1) * TILE_PTS, :].T, fbuf[i])
+        acc_ref[...] = value if i == 0 else acc_ref[...] + value
+        wide = fbuf[i].astype(jnp.float32)
+        squares[0] = squares[0] + jnp.sum((wide * wide).reshape(-1, SUB, wide.shape[1]), axis=0)
+
     core, coords = place()
     partner = device_at(1 - core, coords)
     enter(core, coords)
@@ -158,6 +185,7 @@
         ])
     x, y, z = coords
     out_ref[y, core, x, z] = own_ref[...]
+    add_chunk(0)
     second = []
     for p, ((order, _, _), (low, _, high)) in enumerate(zip(PARTS, SPANS)):
         for copy in first[p]:
@@ -166,6 +194,8 @@
         second.append([
             push(block, device_at(core, coords, order[1], o)) for o in (2, 1, 3)
         ])
+    add_chunk(1)
+    add_chunk(2)
     third, across = [], []
     for p, ((order, _, _), (low, mid, high)) in enumerate(zip(PARTS, SPANS)):
         for copy in second[p]:
@@ -178,6 +208,9 @@
         left_low = push(halves[0], left)
         third.append((right_low, left_high, right_high, left_low))
         across.append(push(region(low, high, order[:2]), partner))
+    add_chunk(3)
+    norms = jnp.sum(squares[0], axis=0, keepdims=True)
+    put_blocks(acc_ref[...], norms, cross_ref, norm_ref)
     relays = []
     for p, ((order, _, _), (low, mid, high)) in enumerate(zip(PARTS, SPANS)):
         axis = order[2]
@@ -206,59 +239,112 @@
         copy.wait_send()
 
 
-def gather_call(own):
+def gather_call(own, targets, factor):
     copies = 9 + 9 + 12 + 3 + 6 + 6 + 6
-    out = pl.pallas_call(
+    pts, held = factor.shape
+    wanted, tiles, steps = targets.shape[1], held // 128, pts // TILE_PTS
+    bf, f32, vmem = jnp.bfloat16, jnp.float32, pltpu.VMEM
+    out, cross, norms = pl.pallas_call(
         gather_kernel,
-        out_shape=jax.ShapeDtypeStruct((4, 2, 4, 4, *own.shape), own.dtype),
-        in_specs=[pl.BlockSpec(memory_space=pltpu.VMEM)],
-        out_specs=pl.BlockSpec(memory_space=pltpu.VMEM),
-        scratch_shapes=[pltpu.SemaphoreType.DMA((copies,))] * 2,
-        compiler_params=pltpu.CompilerParams(collective_id=2, has_side_effects=True),
+        out_shape=(
+            jax.ShapeDtypeStruct((4, 2, 4, 4, *own.shape), bf),
+            jax.ShapeDtypeStruct((2, tiles * 8, 16, 128), bf),
+            jax.ShapeDtypeStruct((tiles, 128), f32),
+        ),
+        in_specs=[pl.BlockSpec(memory_space=vmem)] * 2 + [pl.BlockSpec(memory_space=pl.ANY)],
+        out_specs=[pl.BlockSpec(memory_space=vmem)] * 3,
+        scratch_shapes=[
+            vmem((steps, TILE_PTS, held), bf),
+            vmem((wanted, held), f32),
+            pltpu.SemaphoreType.DMA((copies,)),
+            pltpu.SemaphoreType.DMA((copies,)),
+            pltpu.SemaphoreType.DMA((steps,)),
+        ],
+        compiler_params=pltpu.CompilerParams(
+            collective_id=2, has_side_effects=True, vmem_limit_bytes=48 << 20
+        ),
         name="gather_rows",
-    )(own)
-    return out.reshape(128, *own.shape)
+    )(own, targets, factor)
+    return out.reshape(128, *own.shape), cross, norms
+
+
+MICRO = 16
+
+
+def eliminate(rows, first):
+    groups = len(rows)
+    sub = lax.broadcasted_iota(jnp.int32, (SUB, PANEL), 0)
+    rows = [list(values) for values in rows]
+
+    def over_sublanes(value, k):
+        return jnp.broadcast_to(value[k : k + 1, :], (SUB, PANEL))
+
+    for m in range(0, groups, MICRO // SUB):
+        cols = {}
+        for r in range(m, groups):
+            for k in range(MICRO):
+                lane = first + m * SUB + k
+                cols[r, k] = jnp.broadcast_to(rows[r][0][:, lane : lane + 1], (SUB, PANEL))
+        for k in range(MICRO):
+            g, at = m + k // SUB, k % SUB
+            if at == 0:
+                roots = jnp.ones((SUB, PANEL), jnp.float32)
+            root = lax.rsqrt(over_sublanes(cols[g, k], at))
+            roots = jnp.where(sub == at, root, roots)
+            scale = root * root
+            ahead = {j: over_sublanes(cols[g, j], at) for j in range(k + 1, MICRO)}
+            pivot_rows = [over_sublanes(value, at) for value in rows[g]]
+            for r in range(g, groups):
+                if r == g and at == SUB - 1:
+                    continue
+                c = cols[r, k] * scale
+                if r == g:
+                    c = jnp.where(sub > at, c, 0.0)
+                for j in range(k + 1, MICRO):
+                    cols[r, j] = cols[r, j] - c * ahead[j]
+                rows[r] = [value - c * row for value, row in zip(rows[r], pivot_rows)]
+            if at == SUB - 1:
+                rows[g] = [value * roots for value in rows[g]]
+    return rows
 
 
 def panel_inverse(block):
-    groups = PANEL // SUB
+    half, groups = PANEL // 2, PANEL // 2 // SUB
     sub = lax.broadcasted_iota(jnp.int32, (SUB, PANEL), 0)
     lane = lax.broadcasted_iota(jnp.int32, (SUB, PANEL), 1)
-    rows = [block[SUB * r : SUB * (r + 1), :] for r in range(groups)]
-    inv = [(lane == sub + SUB * r).astype(jnp.float32) for r in range(groups)]
-
-    def over_sublanes(value, k):
-        return jnp.broadcast_to(value[k : k + 1, :], (SUB, PANEL))
-
-    for m in range(groups):
-        live = range(m, groups)
-        cols = {
-            (r, k): jnp.broadcast_to(
-                rows[r][:, SUB * m + k : SUB * m + k + 1], (SUB, PANEL)
-            )
-            for r in live
-            for k in range(SUB)
-        }
-        pivots = jnp.ones((SUB, PANEL), jnp.float32)
-        for k in range(SUB):
-            pivot = over_sublanes(cols[m, k], k)
-            pivots = jnp.where(sub == k, pivot, pivots)
-            scale = 1.0 / pivot
-            ahead = {j: over_sublanes(cols[m, j], k) for j in range(k + 1, SUB)}
-            row, inv_row = over_sublanes(rows[m], k), over_sublanes(inv[m], k)
-            for r in live:
-                c = cols[r, k] * scale
-                if r == m:
-                    c = jnp.where(sub > k, c, 0.0)
-                for j in range(k + 1, SUB):
-                    cols[r, j] = cols[r, j] - c * ahead[j]
-                rows[r] = rows[r] - c * row
-                inv[r] = inv[r] - c * inv_row
-        inv[m] = inv[m] * lax.rsqrt(pivots)
-    return jnp.concatenate(inv, axis=0)
-
-
-def factor_kernel(pad_ref, pos_ref, ps_ref, pf_ref, hi_ref, lo_ref, a_ref, w_ref, sel_ref):
+
+    def unit(row):
+        return (lane == sub + row).astype(jnp.float32)
+
+    pieces = [block[SUB * r : SUB * (r + 1), :] for r in range(2 * groups)]
+    top = eliminate([(pieces[r], unit(SUB * r)) for r in range(groups)], 0)
+    right = jnp.concatenate([values[0] for values in top], axis=0)
+    upper = jnp.concatenate([values[1] for values in top], axis=0)
+    wide = lax.broadcasted_iota(jnp.int32, (half, PANEL), 1)
+    both = jnp.where(wide < half, upper, right)
+    change = jnp.dot(right.T, both, precision=HIGHEST, preferred_element_type=jnp.float32)
+    low = []
+    for r in range(groups, 2 * groups):
+        piece = jnp.where(lane < half, 0.0, pieces[r])
+        low.append((piece - change[SUB * r : SUB * (r + 1), :], unit(SUB * r)))
+    low = eliminate(low, half)
+    lower = [jnp.where(lane < half, values[0], values[1]) for values in low]
+    return jnp.concatenate([upper, *lower], axis=0)
+
+
+def local_kernel(
+    pad_ref, pos_ref, targets_ref, points_ref, factor_ref,
+    new_ref, cross_ref, norm_ref,
+    ps_ref, pf_ref, sel_ref, a_ref, w_ref, lo_ref, hi_ref, down_hi, down_lo, fbuf, fsem,
+):
+    tiles = fbuf.shape[0]
+    copies = []
+    for i in range(tiles):
+        at = pl.ds(i * TILE_PTS, TILE_PTS)
+        copy = pltpu.make_async_copy(factor_ref.at[at, :], fbuf.at[i], fsem.at[i])
+        copy.start()
+        copies.append(copy)
+
     padded = pos_ref.shape[1]
     sel_ref[...] = jnp.where(
         lax.broadcasted_iota(jnp.int32, (BLOCK, padded), 0) == pos_ref[...], 1.0, 0.0
@@ -274,162 +360,117 @@
             ps_ref[:, t * 128 : (t + 2) * 128] = rows
         else:
             pf_ref[:, (t - ahead) * 128 : (t - ahead + 2) * 128] = rows
+
+    panels = BLOCK // PANEL
     total = jnp.zeros((1, BLOCK), jnp.float32)
-    for r in range(BLOCK // PANEL):
+    for r in range(panels):
         at = slice(r * PANEL, (r + 1) * PANEL)
         inter = dot_nt(pf_ref[at, :], pf_ref[...])
         total = total + jnp.sum(jnp.abs(inter), axis=0, keepdims=True)
         kern = jnp.exp(dot_nt(ps_ref[at, :], ps_ref[...]) / ps_ref.shape[1] - 1.0)
         a_ref[at, :] = kern - inter
     shift = ridge_shift + jnp.max(total)
-    row_ids = lax.broadcasted_iota(jnp.int32, (PANEL, BLOCK), 0)
-    lane_ids = lax.broadcasted_iota(jnp.int32, (PANEL, BLOCK), 1)
-    for r in range(BLOCK // PANEL):
-        at = slice(r * PANEL, (r + 1) * PANEL)
-        eye = lane_ids == row_ids + r * PANEL
-        a_ref[at, :] = a_ref[at, :] + jnp.where(eye, shift, 0.0)
-        w_ref[at, :] = jnp.where(eye, 1.0, 0.0)
-
-    @pl.loop(0, BLOCK // PANEL)
-    def _(j):
-        start = pl.multiple_of(j * PANEL, PANEL)
-        at = pl.ds(start, PANEL)
-        inv = panel_inverse(a_ref[at, at])
-        right = jnp.dot(inv, a_ref[at, :], precision=HIGHEST, preferred_element_type=jnp.float32)
-        right = jnp.where(lane_ids >= start + PANEL, right, 0.0)
-        done = jnp.dot(inv, w_ref[at, :], precision=HIGHEST, preferred_element_type=jnp.float32)
-        w_ref[at, :] = done
-        for r in range(1, BLOCK // PANEL):
-            rows = slice(r * PANEL, (r + 1) * PANEL)
-
-            @pl.when(j < r)
-            def _():
-                left = right[:, rows].T
-                a_ref[rows, :] = a_ref[rows, :] - jnp.dot(
-                    left, right, precision=HIGHEST, preferred_element_type=jnp.float32
-                )
-                w_ref[rows, :] = w_ref[rows, :] - jnp.dot(
-                    left, done, precision=HIGHEST, preferred_element_type=jnp.float32
-                )
-
-    high = w_ref[...].astype(jnp.bfloat16)
-    hi_ref[...] = high
-    lo_ref[...] = (w_ref[...] - high.astype(jnp.float32)).astype(jnp.bfloat16)
-
-
-def block_factor(padded, positions, features):
-    held = padded.shape[1] * 128 - features
-    bf = jnp.bfloat16
+    eye = lax.broadcasted_iota(jnp.int32, (PANEL, PANEL), 0) == lax.broadcasted_iota(
+        jnp.int32, (PANEL, PANEL), 1
+    )
+    for copy in copies:
+        copy.wait()
+
+    def exact(a, b):
+        return jnp.dot(a, b, precision=HIGHEST, preferred_element_type=jnp.float32)
+
+    for j in range(panels):
+        at = slice(j * PANEL, (j + 1) * PANEL)
+        inv = panel_inverse(a_ref[at, at] + jnp.where(eye, shift, 0.0))
+        if j:
+            done = jnp.concatenate([exact(inv, w_ref[at, : j * PANEL]), inv], axis=1)
+        else:
+            done = inv
+        high = done.astype(jnp.bfloat16)
+        hi_ref[at, : (j + 1) * PANEL] = high
+        lo_ref[at, : (j + 1) * PANEL] = (done - high.astype(jnp.float32)).astype(jnp.bfloat16)
+        if j + 1 < panels:
+            rest = slice((j + 1) * PANEL, BLOCK)
+            hi_ref[at, rest] = jnp.zeros((PANEL, BLOCK - (j + 1) * PANEL), jnp.bfloat16)
+            lo_ref[at, rest] = jnp.zeros((PANEL, BLOCK - (j + 1) * PANEL), jnp.bfloat16)
+            right = exact(inv, a_ref[at, rest])
+            for r in range(j + 1, panels):
+                rows = slice(r * PANEL, (r + 1) * PANEL)
+                skip = (r - j - 1) * PANEL
+                left = right[:, skip : skip + PANEL].T
+                a_ref[rows, r * PANEL :] = a_ref[rows, r * PANEL :] - exact(left, right[:, skip:])
+                gone = exact(left, done)
+                if j:
+                    w_ref[rows, : j * PANEL] = w_ref[rows, : j * PANEL] - gone[:, : j * PANEL]
+                w_ref[rows, at] = -gone[:, j * PANEL :]
+        tile = slice(j * TILE_PTS, (j + 1) * TILE_PTS)
+        scaled = normalize(points_ref[tile, :])
+        down = jnp.exp(dot_nt(ps_ref[...], scaled) / scaled.shape[1] - 1.0) - dot_nt(
+            pf_ref[...], fbuf[j]
+        )
+        high = down.astype(jnp.bfloat16)
+        down_hi[:, tile] = high
+        down_lo[:, tile] = (down - high.astype(jnp.float32)).astype(jnp.bfloat16)
+
+    half = BLOCK // 2
+    wanted = targets_ref.shape[1]
+    acc = jnp.zeros((wanted, BLOCK), jnp.float32)
+    nsq = jnp.zeros((BLOCK, 128), jnp.float32)
+    for i in range(tiles):
+        tile = slice(i * TILE_PTS, (i + 1) * TILE_PTS)
+        for top, wide in ((0, half), (half, BLOCK)):
+            at = slice(top, top + half)
+            value = (
+                dot_nn(hi_ref[at, :wide], down_hi[:wide, tile])
+                + dot_nn(hi_ref[at, :wide], down_lo[:wide, tile])
+                + dot_nn(lo_ref[at, :wide], down_hi[:wide, tile])
+            )
+            new_ref[at, tile] = value.astype(jnp.bfloat16)
+        new = new_ref[:, tile]
+        acc = acc + dot_nt(targets_ref[tile, :].T, new)
+        wide_new = new.astype(jnp.float32)
+        squares = wide_new * wide_new
+        for t in range(TILE_PTS // 128):
+            nsq = nsq + squares[:, t * 128 : (t + 1) * 128]
+    norms = jnp.sum(nsq.T, axis=0, keepdims=True)
+    put_blocks(acc, norms, cross_ref, norm_ref)
+
+
+def local_call(padded, positions, points, factor, targets):
+    pts, held = factor.shape
+    features = points.shape[1]
+    tiles = BLOCK // 128
+    bf, f32, vmem = jnp.bfloat16, jnp.float32, pltpu.VMEM
+    steps = pts // TILE_PTS
     return pl.pallas_call(
-        factor_kernel,
+        local_kernel,
         out_shape=(
-            jax.ShapeDtypeStruct((BLOCK, features), bf),
-            jax.ShapeDtypeStruct((BLOCK, held), bf),
-            jax.ShapeDtypeStruct((BLOCK, BLOCK), bf),
-            jax.ShapeDtypeStruct((BLOCK, BLOCK), bf),
+            jax.ShapeDtypeStruct((BLOCK, pts), bf),
+            jax.ShapeDtypeStruct((2, tiles * 8, 16, 128), bf),
+            jax.ShapeDtypeStruct((tiles, 128), f32),
         ),
-        in_specs=[pl.BlockSpec(memory_space=pltpu.VMEM)] * 2,
-        out_specs=[pl.BlockSpec(memory_space=pltpu.VMEM)] * 4,
-        scratch_shapes=[pltpu.VMEM((BLOCK, BLOCK), jnp.float32)] * 2
-        + [pltpu.VMEM((BLOCK, positions.shape[1]), bf)],
-        name="block_factor",
-    )(padded, positions)
-
-
-def columns_kernel(
-    points_ref, factor_ref, targets_ref, ps_ref, pf_ref, hi_ref, lo_ref,
-    new_ref, cross_ref, norm_ref, acc_ref, fsq_ref, nsq_ref,
-):
-    step = pl.program_id(0)
-    held = factor_ref.shape[1]
-
-    @pl.when(step == 0)
-    def _():
-        acc_ref[...] = jnp.zeros_like(acc_ref)
-        fsq_ref[...] = jnp.zeros_like(fsq_ref)
-        nsq_ref[...] = jnp.zeros_like(nsq_ref)
-
-    scaled = normalize(points_ref[...])
-    factor = factor_ref[...]
-    down = jnp.exp(dot_nt(ps_ref[...], scaled) / scaled.shape[1] - 1.0) - dot_nt(
-        pf_ref[...], factor
-    )
-    down_hi = down.astype(jnp.bfloat16)
-    down_lo = (down - down_hi.astype(jnp.float32)).astype(jnp.bfloat16)
-    half = BLOCK // 2
-    for top, wide in ((0, half), (half, BLOCK)):
-        at = slice(top, top + half)
-        new_ref[at, :] = (
-            dot_nn(hi_ref[at, :wide], down_hi[:wide])
-            + dot_nn(hi_ref[at, :wide], down_lo[:wide])
-            + dot_nn(lo_ref[at, :wide], down_hi[:wide])
-        ).astype(jnp.bfloat16)
-    new = new_ref[...]
-    turned = targets_ref[...].T
-    acc_ref[:, :held] += dot_nn(turned, factor)
-    acc_ref[:, held:] += dot_nt(turned, new)
-    wide_factor = factor.astype(jnp.float32)
-    fsq_ref[...] += jnp.sum(
-        (wide_factor * wide_factor).reshape(-1, SUB, held), axis=0
-    )
-    wide_new = new.astype(jnp.float32)
-    squares = wide_new * wide_new
-    nsq = nsq_ref[...]
-    for t in range(new.shape[1] // 128):
-        nsq = nsq + squares[:, t * 128 : (t + 1) * 128]
-    nsq_ref[...] = nsq
-
-    @pl.when(step == pl.num_programs(0) - 1)
-    def _():
-        held_norm = jnp.sum(fsq_ref[...], axis=0, keepdims=True)
-        new_norm = jnp.sum(nsq_ref[...].T, axis=0, keepdims=True)
-        norms = jnp.concatenate([held_norm, new_norm], axis=1)
-        for t in range(norms.shape[1] // 128):
-            lanes = slice(t * 128, (t + 1) * 128)
-            norm_ref[t : t + 1, :] = norms[:, lanes]
-            piece = acc_ref[:, lanes].astype(jnp.bfloat16)
-            cross_ref[:, t * 8 : (t + 1) * 8] = piece.reshape(2, 8, 16, 128)
-
-
-def columns_call(points, factor, targets, pivot_scaled, pivot_factor, inv_hi, inv_lo):
-    pts, held = factor.shape
-    features, wanted = points.shape[1], targets.shape[1]
-    tiles = (held + BLOCK) // 128
-    whole = lambda i: (0, 0)
-    once = pl.Buffered(1)
-    return pl.pallas_call(
-        columns_kernel,
-        grid=(pts // TILE_PTS,),
-        out_shape=(
-            jax.ShapeDtypeStruct((BLOCK, pts), jnp.bfloat16),
-            jax.ShapeDtypeStruct((2, tiles * 8, 16, 128), jnp.bfloat16),
-            jax.ShapeDtypeStruct((tiles, 128), jnp.float32),
-        ),
-        in_specs=[
-            pl.BlockSpec((TILE_PTS, features), lambda i: (i, 0)),
-            pl.BlockSpec((TILE_PTS, held), lambda i: (i, 0)),
-            pl.BlockSpec((TILE_PTS, wanted), lambda i: (i, 0)),
-            pl.BlockSpec((BLOCK, features), whole, pipeline_mode=once),
-            pl.BlockSpec((BLOCK, held), whole, pipeline_mode=once),
-            pl.BlockSpec((BLOCK, BLOCK), whole, pipeline_mode=once),
-            pl.BlockSpec((BLOCK, BLOCK), whole, pipeline_mode=once),
+        in_specs=[pl.BlockSpec(memory_space=vmem)] * 4 + [pl.BlockSpec(memory_space=pl.ANY)],
+        out_specs=[pl.BlockSpec(memory_space=vmem)] * 3,
+        scratch_shapes=[
+            vmem((BLOCK, features), bf),
+            vmem((BLOCK, held), bf),
+            vmem((BLOCK, positions.shape[1]), bf),
+            vmem((BLOCK, BLOCK), f32),
+            vmem((BLOCK, BLOCK), f32),
+            vmem((BLOCK, BLOCK), bf),
+            vmem((BLOCK, BLOCK), bf),
+            vmem((BLOCK, pts), bf),
+            vmem((BLOCK, pts), bf),
+            vmem((steps, TILE_PTS, held), bf),
+            pltpu.SemaphoreType.DMA((steps,)),
         ],
-        out_specs=[
-            pl.BlockSpec((BLOCK, TILE_PTS), lambda i: (0, i)),
-            pl.BlockSpec((2, tiles * 8, 16, 128), lambda i: (0, 0, 0, 0)),
-            pl.BlockSpec((tiles, 128), whole),
-        ],
-        scratch_shapes=[
-            pltpu.VMEM((wanted, held + BLOCK), jnp.float32),
-            pltpu.VMEM((SUB, held), jnp.float32),
-            pltpu.VMEM((BLOCK, 128), jnp.float32),
-        ],
-        name="new_columns",
-    )(points, factor, targets, pivot_scaled, pivot_factor, inv_hi, inv_lo)
+        compiler_params=pltpu.CompilerParams(vmem_limit_bytes=44 << 20),
+        name="local_block",
+    )(padded, positions, targets, points, factor)
 
 
 def sums_kernel(
-    x_ref, n_ref, out_ref, got0, sum0, out0, norm_got0, norm_sum, norm_got, coef, got_last,
+    xf_ref, xn_ref, nf_ref, nn_ref, out_ref, got0, sum0, out0, norm_got0, norm_sum, norm_got, coef, got_last,
     a0, a1, a2, b0, b1, b2, c0, c1, c2, s1, s2, s3, t1, t2, t3, u1, u2, u3,
     send, recv,
 ):
@@ -457,13 +498,21 @@
     wide = lambda v: v.astype(jnp.float32)
     narrow = lambda v: v.astype(jnp.bfloat16)
 
+    split, tiles = xf_ref.shape[1], nf_ref.shape[0]
     arrive([
-        start(x_ref.at[1 - core], got0, partner),
-        start(n_ref, norm_got0, partner),
+        start(xf_ref.at[1 - core], got0.at[:split], partner),
+        start(xn_ref.at[1 - core], got0.at[split:], partner),
+        start(nf_ref, norm_got0.at[:tiles], partner),
+        start(nn_ref, norm_got0.at[tiles : tiles + nn_ref.shape[0]], partner),
     ])
-    sum0[...] = wide(x_ref[core]) + wide(got0[...])
-    out0[...] = narrow(sum0[...])
-    norm_sum[0] = n_ref[...] + norm_got0[...]
+    for src, at in ((xf_ref, slice(0, split)), (xn_ref, slice(split, got0.shape[0]))):
+        value = wide(src[core]) + wide(got0[at])
+        sum0[at] = value
+        out0[at] = narrow(value)
+    last_tile = tiles + nn_ref.shape[0]
+    norm_sum[0, :tiles] = nf_ref[...] + norm_got0[:tiles]
+    norm_sum[0, tiles:last_tile] = nn_ref[...] + norm_got0[tiles:last_tile]
+    norm_sum[0, last_tile:] = jnp.zeros_like(norm_sum[0, last_tile:])
 
     got = ((a0, a1, a2), (b0, b1, b2), (c0, c1, c2))
     sums = ((s1, s2, s3), (t1, t2, t3))
@@ -571,8 +620,9 @@
         copy.wait_send()
 
 
-def sums_call(cross, norms):
-    blocks, tiles = cross.shape[1], norms.shape[0]
+def sums_call(cross_f, cross_n, norms_f, norms_n):
+    blocks = cross_f.shape[1] + cross_n.shape[1]
+    tiles = 24
     bf, f32, vmem = jnp.bfloat16, jnp.float32, pltpu.VMEM
     piece = lambda lead, n, kind: vmem((*lead, n, 16, 128), kind)
     sizes = [size for _, _, size in PARTS]
@@ -587,17 +637,19 @@
     scratch += [piece((), s // 4, f32) for s in sizes]
     scratch += [piece((1,), s // 16, f32) for s in sizes]
     scratch += [piece((), s // 4, bf) for s in sizes]
-    copies = 2 + 12 * 3 + 9 * 2 + 1
+    copies = 4 + 12 * 3 + 9 * 2 + 1
     scratch += [pltpu.SemaphoreType.DMA((copies,))] * 2
     return pl.pallas_call(
         sums_kernel,
-        out_shape=jax.ShapeDtypeStruct(cross.shape, bf),
-        in_specs=[pl.BlockSpec(memory_space=vmem)] * 2,
+        out_shape=jax.ShapeDtypeStruct((2, blocks, 16, 128), bf),
+        in_specs=[pl.BlockSpec(memory_space=vmem)] * 4,
         out_specs=pl.BlockSpec(memory_space=vmem),
         scratch_shapes=scratch,
-        compiler_params=pltpu.CompilerParams(collective_id=1, has_side_effects=True),
+        compiler_params=pltpu.CompilerParams(
+            collective_id=1, has_side_effects=True, vmem_limit_bytes=24 << 20
+        ),
         name="sums",
-    )(cross, norms)
+    )(cross_f, cross_n, norms_f, norms_n)
 
 
 def residual_kernel(factor_ref, new_ref, targets_ref, coef_ref, out_ref, turned_ref):
@@ -629,21 +681,17 @@
         ],
         out_specs=pl.BlockSpec((TILE_PTS, wanted), lambda i: (i, 0)),
         scratch_shapes=[pltpu.VMEM((wanted, held + BLOCK), jnp.bfloat16)],
+        compiler_params=pltpu.CompilerParams(vmem_limit_bytes=24 << 20),
         name="residual",
     )(factor, new, targets, coef)
 
 
 def on_device(points, factor, targets, pivot_slots, pivot_counts):
     own = rows_call(pivot_slots, points, factor)
-    padded = gather_call(own)
+    padded, cross_f, norms_f = gather_call(own, targets, factor)
     positions = padded_positions(pivot_counts, pivot_slots.shape[1])
-    pivot_scaled, pivot_factor, inv_hi, inv_lo = block_factor(
-        padded, positions, points.shape[1]
-    )
-    new_columns, cross, norms = columns_call(
-        points, factor, targets, pivot_scaled, pivot_factor, inv_hi, inv_lo
-    )
-    coef = sums_call(cross, norms)
+    new_columns, cross_n, norms_n = local_call(padded, positions, points, factor, targets)
+    coef = sums_call(cross_f, cross_n, norms_f, norms_n)
     residual_next = residual_call(factor, new_columns, targets, coef)
     return (new_columns, residual_next)
 

time: 128 us -> 102 us (0.80)
  Pallas kernels: 125 us -> 97.3 us
  local copies, waits for them, and re-layouts: 0.81 us -> 3.64 us
    pallas_call x4 -> x3, Pallas kernels: 114 us -> 89.9 us  [the longest x1 30.9 us: gather_call(): pl.pallas_call(gather_kernel, out_shape=(jax.ShapeDtypeStruct((4, 2, 4, 4...]
    pallas_call x1, Pallas kernels: 8.25 us -> 4.65 us  [residual_call(): pl.pallas_call(residual_kernel, grid=(pts // TILE_PTS,), out_shape=jax.Sh...]
    unnamed x2 -> x16, local copies, waits for them, and re-layouts: 0.01 us -> 3.43 us
where the time goes in v3:
time: 102 us
  Pallas kernels  97.3 us (95%)
  local copies, waits for them, and re-layouts  3.64 us (4%)
    pallas_call x1, Pallas kernels, gather_call(): pl.pallas_call(gather_kernel, out_shape=(jax.ShapeDtypeStruct((4, 2, 4, 4...  30.9 us
    pallas_call x1, Pallas kernels, sums_call(): pl.pallas_call(sums_kernel, out_shape=jax.ShapeDtypeStruct((2, blocks, 16...  29.6 us
    pallas_call x1, Pallas kernels, local_call(): pl.pallas_call(local_kernel, out_shape=(jax.ShapeDtypeStruct((BLOCK, pts)...  29.4 us
    pallas_call x1, Pallas kernels, residual_call(): pl.pallas_call(residual_kernel, grid=(pts // TILE_PTS,), out_shape=jax.Sh...  4.65 us
    unnamed x16, local copies, waits for them, and re-layouts  3.43 us
    pallas_call x1, Pallas kernels, rows_call(): pl.pallas_call(rows_kernel, out_shape=jax.ShapeDtypeStruct(((features + h...  2.73 us

profile of v3, /device:TPU:1, one launch (start us, length us, event | category | flops | bytes accessed | tf_op | source)
XLA Modules:
  0.0 102.1 jit_solution(8019794199944735337)
XLA Ops:
  0.6 0.0 copy-start.5
  0.6 0.0 copy-start
  0.7 2.7 %pivot_rows.1.own_ref = bf16[20,8,128]{2,1,0:T(8,128)(2,1)} custom-call(s32[1,8]{1,0:T(1,128)} %slots_ref.1, bf16[2048,512]{1,0:T(8,128)(2,1)} %points_ref.3, bf16[2048,2048]{1,0:T(8,128)(2,1)} %factor_ref.7), custom_call_target="tpu_custom_call" | custom-call | tf_op jit(solution)/shard_map/pivot_rows/pallas_call | solution.py:112
  3.4 0.0 copy-done.5
  3.4 0.1 copy.8
  3.5 0.2 reduce-window.9
  3.7 0.1 reduce
  3.8 0.1 add_select_fusion
  3.9 0.1 select_n.15.pos_ref
  4.0 0.0 copy-done
  4.0 0.0 copy-start.4
  4.0 0.8 copy-done.4
  4.8 0.0 copy-start.1
  4.8 30.9 %gather_rows.1 = (bf16[4,2,4,4,20,8,128]{6,5,4,3,2,1,0:T(8,128)(2,1)}, bf16[2,128,16,128]{3,2,1,0:T(8,128)(2,1)S(1)}, f32[16,128]{1,0:T(8,128)S(1)}) custom-call(bf16[20,8,128]{2,1,0:T(8,128)(2,1)S(1)} %copy-done.4, bf16[2048,256]{1,0:T(8,128)(2,1)S(1)} %copy-done, bf16[2048,2048]{1,0:T(8,128)(2,1)} %factor_ref.7), custom_call_target="tpu_custom_call" | custom-call | tf_op jit(solution)/shard_map/gather_rows/pallas_call | solution.py:247
  35.7 0.0 slice-start
  35.7 0.0 copy-done.1
  35.7 0.0 copy-start.2
  35.7 2.6 %copy-done.2 = bf16[4,2,4,4,20,8,128]{6,5,4,3,2,1,0:T(8,128)(2,1)S(1)} copy-done((bf16[4,2,4,4,20,8,128]{6,5,4,3,2,1,0:T(8,128)(2,1)S(1)}, bf16[4,2,4,4,20,8,128]{6,5,4,3,2,1,0:T(8,128)(2,1)}, u32[]{:S(2)}) %copy-start.2) | copy-done | bytes 5242904
  38.4 0.0 slice-start.1
  38.4 29.4 %local_block.1 = (bf16[512,2048]{1,0:T(8,128)(2,1)}, bf16[2,32,16,128]{3,2,1,0:T(8,128)(2,1)S(1)}, f32[4,128]{1,0:T(4,128)S(1)}) custom-call(bf16[128,20,8,128]{3,2,1,0:T(8,128)(2,1)S(1)} %bitcast.4, s32[1,1024]{1,0:T(1,128)S(1)} %select_n.15.pos_ref, bf16[2048,256]{1,0:T(8,128)(2,1)S(1)} %copy-done, bf16[2048,512]{1,0:T(8,128)(2,1)S(1)} %copy-done.1, ...), custom_call_target="tpu_custom_call" | custom-call | tf_op jit(solution)/shard_map/local_block/pallas_call | solution.py:445
  67.8 0.0 copy-start.3
  67.8 29.6 %sums.1.coef_ref = bf16[2,160,16,128]{3,2,1,0:T(8,128)(2,1)S(1)} custom-call(bf16[2,128,16,128]{3,2,1,0:T(8,128)(2,1)S(1)} %get-tuple-element.10.xf_ref, bf16[2,32,16,128]{3,2,1,0:T(8,128)(2,1)S(1)} %get-tuple-element.11.xn_ref, f32[16,128]{1,0:T(8,128)S(1)} %get-tuple-element.12.nf_ref, f32[4,128]{1,0:T(4,128)S(1)} %get-tuple-element.13.nn_ref), custom_call_target="tpu_custom_call" | custom-call | tf_op jit(solution)/shard_map/sums/pallas_call | solution.py:642
  97.4 0.0 slice-done
  97.4 0.0 slice-done.1
  97.4 0.0 copy-done.3
  97.5 4.6 %residual.1 = f32[2048,256]{1,0:T(8,128)} custom-call(bf16[2048,2048]{1,0:T(8,128)(2,1)S(1)} %bitcast.3, bf16[512,2048]{1,0:T(8,128)(2,1)S(1)} %copy-done.3, bf16[2048,256]{1,0:T(8,128)(2,1)S(1)} %copy-done, bf16[2,160,16,128]{3,2,1,0:T(8,128)(2,1)S(1)} %sums.1.coef_ref), custom_call_target="tpu_custom_call" | custom-call | tf_op jit(solution)/shard_map/residual/pallas_call | solution.py:672
  (2 shorter events, 0.0 us)
Async XLA Ops:
  0.6 2.8 %copy-start.5 = (s32[128]{0:T(128)S(1)}, s32[128]{0:T(128)}, u32[]{:S(2)}) copy-start(s32[128]{0:T(128)} %param.9) | copy-start | bytes 1540
  0.6 3.4 %copy-start = (bf16[2048,256]{1,0:T(8,128)(2,1)S(1)}, bf16[2048,256]{1,0:T(8,128)(2,1)}, u32[]{:S(2)}) copy-start(bf16[2048,256]{1,0:T(8,128)(2,1)} %targets_ref.5) | copy-start | bytes 3145732
  4.0 0.8 copy-start.4
  4.8 30.9 %copy-start.1 = (bf16[2048,512]{1,0:T(8,128)(2,1)S(1)}, bf16[2048,512]{1,0:T(8,128)(2,1)}, u32[]{:S(2)}) copy-start(bf16[2048,512]{1,0:T(8,128)(2,1)} %points_ref.3) | copy-start | bytes 6291460
  35.7 61.7 %slice-start = ((s8[8388608]{0:T(1024)(128)(4,1)}), s8[4194304]{0:T(1024)(128)(4,1)S(1)}, s32[]{:S(2)}) async-start(s8[8388608]{0:T(1024)(128)(4,1)} %bitcast.2), calls=%async_computation | async-start | bytes 8388608
  35.7 2.6 %copy-start.2 = (bf16[4,2,4,4,20,8,128]{6,5,4,3,2,1,0:T(8,128)(2,1)S(1)}, bf16[4,2,4,4,20,8,128]{6,5,4,3,2,1,0:T(8,128)(2,1)}, u32[]{:S(2)}) copy-start(bf16[4,2,4,4,20,8,128]{6,5,4,3,2,1,0:T(8,128)(2,1)} %get-tuple-element.8) | copy-start | bytes 15728644
  38.4 59.1 %slice-start.1 = ((s8[8388608]{0:T(1024)(128)(4,1)}), s8[4194304]{0:T(1024)(128)(4,1)S(1)}, s32[]{:S(2)}) async-start(s8[8388608]{0:T(1024)(128)(4,1)} %bitcast.2), calls=%async_computation.1 | async-start | bytes 8388608
  67.8 29.6 %copy-start.3 = (bf16[512,2048]{1,0:T(8,128)(2,1)S(1)}, bf16[512,2048]{1,0:T(8,128)(2,1)}, u32[]{:S(2)}) copy-start(bf16[512,2048]{1,0:T(8,128)(2,1)} %get-tuple-element.6.new_ref) | copy-start | bytes 6291460

commit v4 on v3

--- a/solution.py
+++ b/solution.py
@@ -11,6 +11,9 @@
 PANEL = 128
 SUB = 8
 TILE_PTS = 512
+ROWS_VMEM, GATHER_VMEM, LOCAL_VMEM, SUMS_VMEM, RESIDUAL_VMEM = (
+    mib << 20 for mib in (60, 40, 38, 16, 16)
+)
 MESH = pl.DeviceIdType.MESH
 HIGHEST = lax.Precision.HIGHEST
 
@@ -49,7 +52,9 @@
         )
 
 
-PARTS = (((0, 1, 2), 0, 64), ((1, 2, 0), 64, 48), ((2, 0, 1), 112, 48))
+ORDERS = ((0, 1, 2), (1, 2, 0), (2, 0, 1))
+HELD_PARTS = ((0, 48), (48, 48), (96, 32))
+NEW_PARTS = ((0, 12), (12, 12), (24, 8))
 
 
 def place():
@@ -73,6 +78,47 @@
     for peer in peers:
         pl.semaphore_signal(barrier, inc=1, device_id=peer, device_id_type=MESH)
     pl.semaphore_wait(barrier, len(peers))
+
+
+def load_tiles(src, buf, sem):
+    loads = []
+    for i in range(buf.shape[0]):
+        tile = src.at[pl.ds(i * TILE_PTS, TILE_PTS), :]
+        loads.append(pltpu.make_async_copy(tile, buf.at[i], sem.at[i]))
+        loads[i].start()
+    return loads
+
+
+class Copies:
+    def __init__(self, send, recv):
+        self.send, self.recv, self.started = send, recv, []
+
+    def start(self, src, dst, device):
+        k = len(self.started)
+        copy = pltpu.make_async_remote_copy(
+            src_ref=src, dst_ref=dst, send_sem=self.send.at[k], recv_sem=self.recv.at[k],
+            device_id=device, device_id_type=MESH,
+        )
+        copy.start()
+        self.started.append(copy)
+        return copy
+
+    def finish(self):
+        for copy in self.started:
+            copy.wait_send()
+
+
+def arrive(copies):
+    for copy in copies:
+        copy.wait_recv()
+
+
+def wide(value):
+    return value.astype(jnp.float32)
+
+
+def narrow(value):
+    return value.astype(jnp.bfloat16)
 
 
 def rows_kernel(slots_ref, points_ref, factor_ref, out_ref, pbuf, fbuf, psem, fsem):
@@ -124,6 +170,7 @@
             pltpu.SemaphoreType.DMA((cap,)),
             pltpu.SemaphoreType.DMA((cap,)),
         ],
+        compiler_params=pltpu.CompilerParams(vmem_limit_bytes=ROWS_VMEM),
         name="pivot_rows",
     )(pivot_slots, points, factor)
 
@@ -132,40 +179,18 @@
 
 
 def gather_kernel(
-    own_ref, targets_ref, factor_ref, out_ref, cross_ref, norm_ref, fbuf, acc_ref, send, recv, fsem
+    own_ref, targets_ref, factor_ref, out_ref, shard_ref, acc_ref, x_ref, n_ref, got0, norm_got0,
+    sum0, out0, norm_sum, norm_got, a0, a1, a2, b0, b1, b2, c0, c1, c2, s0, s1, s2, u0, u1, u2,
+    v0, v1, v2, fbuf, fsem, send, recv,
 ):
-    chunks = fbuf.shape[0]
-    loads = []
-    for i in range(chunks):
-        at = pl.ds(i * TILE_PTS, TILE_PTS)
-        load = pltpu.make_async_copy(factor_ref.at[at, :], fbuf.at[i], fsem.at[i])
-        load.start()
-        loads.append(load)
-    squares = [jnp.zeros((SUB, fbuf.shape[2]), jnp.float32)]
-
-    def add_chunk(i):
-        loads[i].wait()
-        value = dot_nn(targets_ref[i * TILE_PTS : (i + 1) * TILE_PTS, :].T, fbuf[i])
-        acc_ref[...] = value if i == 0 else acc_ref[...] + value
-        wide = fbuf[i].astype(jnp.float32)
-        squares[0] = squares[0] + jnp.sum((wide * wide).reshape(-1, SUB, wide.shape[1]), axis=0)
-
     core, coords = place()
     partner = device_at(1 - core, coords)
+    loads = load_tiles(factor_ref, fbuf, fsem)
     enter(core, coords)
-    count = [0]
-    sent = []
-
-    def start(src, dst, device):
-        k = count[0]
-        count[0] += 1
-        copy = pltpu.make_async_remote_copy(
-            src_ref=src, dst_ref=dst, send_sem=send.at[k], recv_sem=recv.at[k],
-            device_id=device, device_id_type=MESH,
-        )
-        copy.start()
-        sent.append(copy)
-        return copy
+    copies = Copies(send, recv)
+
+    def peer(axis, offset):
+        return device_at(core, coords, axis, offset)
 
     def region(low, high, whole=(), axis=None, at=None):
         x, y, z = (
@@ -175,32 +200,44 @@
         return out_ref.at[y, core, x, z, low:high]
 
     def push(block, device):
-        return start(block, block, device)
+        return copies.start(block, block, device)
 
     first = []
-    for (order, _, _), (low, _, high) in zip(PARTS, SPANS):
+    for order, (low, _, high) in zip(ORDERS, SPANS):
         first.append([
-            start(own_ref.at[low:high], region(low, high), device_at(core, coords, order[0], o))
+            copies.start(own_ref.at[low:high], region(low, high), peer(order[0], o))
             for o in (2, 1, 3)
         ])
     x, y, z = coords
     out_ref[y, core, x, z] = own_ref[...]
-    add_chunk(0)
+    squares = jnp.zeros((SUB, factor_ref.shape[1]), jnp.float32)
+    chunks = factor_ref.shape[0] // TILE_PTS
+
+    def add_chunk(i, squares):
+        at = slice(i * TILE_PTS, (i + 1) * TILE_PTS)
+        loads[i].wait()
+        value = dot_nn(targets_ref[at, :].T, fbuf[i])
+        acc_ref[...] = value if i == 0 else acc_ref[...] + value
+        values = wide(fbuf[i])
+        return squares + jnp.sum((values * values).reshape(-1, SUB, values.shape[1]), axis=0)
+
+    squares = add_chunk(0, squares)
     second = []
-    for p, ((order, _, _), (low, _, high)) in enumerate(zip(PARTS, SPANS)):
-        for copy in first[p]:
-            copy.wait_recv()
+    for p, (order, (low, _, high)) in enumerate(zip(ORDERS, SPANS)):
+        arrive(first[p])
         block = region(low, high, order[:1])
-        second.append([
-            push(block, device_at(core, coords, order[1], o)) for o in (2, 1, 3)
-        ])
-    add_chunk(1)
-    add_chunk(2)
+        second.append([push(block, peer(order[1], o)) for o in (2, 1, 3)])
+    for i in range(1, chunks):
+        squares = add_chunk(i, squares)
+    put_blocks(acc_ref[...], jnp.sum(squares, axis=0, keepdims=True), x_ref, n_ref)
+    zero = [
+        copies.start(x_ref.at[1 - core], got0, partner),
+        copies.start(n_ref, norm_got0, partner),
+    ]
     third, across = [], []
-    for p, ((order, _, _), (low, mid, high)) in enumerate(zip(PARTS, SPANS)):
-        for copy in second[p]:
-            copy.wait_recv()
-        left, right = (device_at(core, coords, order[2], o) for o in (3, 1))
+    for p, (order, (low, mid, high)) in enumerate(zip(ORDERS, SPANS)):
+        arrive(second[p])
+        left, right = peer(order[2], 3), peer(order[2], 1)
         halves = [region(a, b, order[:2]) for a, b in ((low, mid), (mid, high))]
         right_low = push(halves[0], right)
         left_high = push(halves[1], left)
@@ -208,64 +245,148 @@
         left_low = push(halves[0], left)
         third.append((right_low, left_high, right_high, left_low))
         across.append(push(region(low, high, order[:2]), partner))
-    add_chunk(3)
-    norms = jnp.sum(squares[0], axis=0, keepdims=True)
-    put_blocks(acc_ref[...], norms, cross_ref, norm_ref)
+
+    arrive(zero)
+    sum0[...] = wide(x_ref[core]) + wide(got0[...])
+    out0[...] = narrow(sum0[...])
+    norm_sum[0] = n_ref[...] + norm_got0[...]
+    one, starts = [], []
+    for p, (order, (base, size)) in enumerate(zip(ORDERS, HELD_PARTS)):
+        here, piece = coords[order[0]], size // 4
+        for o in range(1, 4):
+            there = lax.rem(here + o, 4)
+            one.append(
+                copies.start(
+                    out0.at[pl.ds(base + there * piece, piece)],
+                    (a0, a1, a2)[p].at[o - 1],
+                    peer(order[0], o),
+                )
+            )
+        starts.append(base + here * piece)
+    for o in range(1, 4):
+        one.append(copies.start(norm_sum.at[0], norm_got.at[0, o - 1], peer(0, o)))
+
     relays = []
-    for p, ((order, _, _), (low, mid, high)) in enumerate(zip(PARTS, SPANS)):
+    for p, (order, (low, mid, high)) in enumerate(zip(ORDERS, SPANS)):
         axis = order[2]
         before, after = (lax.rem(coords[axis] + o, 4) for o in (3, 1))
-        left, right = (device_at(core, coords, axis, o) for o in (3, 1))
         third[p][0].wait_recv()
-        one = push(region(low, mid, order[:2], axis, before), right)
+        relay = push(region(low, mid, order[:2], axis, before), peer(axis, 1))
         third[p][1].wait_recv()
-        relays.append((one, push(region(mid, high, order[:2], axis, after), left)))
-    for p, ((order, _, _), (low, mid, high)) in enumerate(zip(PARTS, SPANS)):
+        relays.append((relay, push(region(mid, high, order[:2], axis, after), peer(axis, 3))))
+
+    arrive(one)
+    two = []
+    for p, (order, (base, size)) in enumerate(zip(ORDERS, HELD_PARTS)):
+        here, piece, fours = coords[order[1]], size // 16, size // 4
+        value = sum0[pl.ds(starts[p], fours)]
+        for o in range(3):
+            value = value + wide((a0, a1, a2)[p][o])
+        (s0, s1, s2)[p][...] = value
+        (u0, u1, u2)[p][...] = narrow(value)
+        for o in range(1, 4):
+            there = lax.rem(here + o, 4)
+            two.append(
+                copies.start(
+                    (u0, u1, u2)[p].at[pl.ds(there * piece, piece)],
+                    (b0, b1, b2)[p].at[o - 1],
+                    peer(order[1], o),
+                )
+            )
+        starts[p] = starts[p] + here * piece
+    norm_sum[1] = norm_sum[0] + norm_got[0, 0] + norm_got[0, 1] + norm_got[0, 2]
+    for o in range(1, 4):
+        two.append(copies.start(norm_sum.at[1], norm_got.at[1, o - 1], peer(1, o)))
+
+    for p, (order, (low, mid, high)) in enumerate(zip(ORDERS, SPANS)):
         axis = order[2]
         before, after = (lax.rem(coords[axis] + o, 4) for o in (3, 1))
         third[p][2].wait_recv()
         across.append(push(region(low, high, order[:2], axis, before), partner))
         third[p][3].wait_recv()
         across.append(push(region(low, high, order[:2], axis, after), partner))
-    for p, ((order, _, _), (low, mid, high)) in enumerate(zip(PARTS, SPANS)):
+
+    arrive(two)
+    three, values = [], []
+    for p, (order, (base, size)) in enumerate(zip(ORDERS, HELD_PARTS)):
+        here, piece = coords[order[1]], size // 16
+        value = (s0, s1, s2)[p][pl.ds(here * piece, piece)]
+        for o in range(3):
+            value = value + wide((b0, b1, b2)[p][o])
+        values.append(value)
+        (v0, v1, v2)[p][...] = narrow(value)
+        for o in range(1, 4):
+            three.append(
+                copies.start((v0, v1, v2)[p], (c0, c1, c2)[p].at[o - 1], peer(order[2], o))
+            )
+    norm_sum[2] = norm_sum[1] + norm_got[1, 0] + norm_got[1, 1] + norm_got[1, 2]
+    for o in range(1, 4):
+        three.append(copies.start(norm_sum.at[2], norm_got.at[2, o - 1], peer(2, o)))
+
+    for p, (order, (low, mid, high)) in enumerate(zip(ORDERS, SPANS)):
         axis = order[2]
         opposite = lax.rem(coords[axis] + 2, 4)
         for copy, (a, b) in zip(relays[p], ((low, mid), (mid, high))):
             copy.wait_recv()
             across.append(push(region(a, b, order[:2], axis, opposite), partner))
-    for copy in across:
-        copy.wait_recv()
-    for copy in sent:
-        copy.wait_send()
+
+    arrive(three)
+    norm_sum[3] = norm_sum[2] + norm_got[2, 0] + norm_got[2, 1] + norm_got[2, 2]
+    at = 0
+    for p, (order, (base, size)) in enumerate(zip(ORDERS, HELD_PARTS)):
+        value = values[p]
+        for o in range(3):
+            value = value + wide((c0, c1, c2)[p][o])
+        for i in range(size // 16):
+            norm = norm_sum[3, pl.ds(lax.div(starts[p] + i, 8), 1), :]
+            shard_ref[at] = narrow(value[i] / (norm + damping))
+            at += 1
+    arrive(across)
+    copies.finish()
+
+
+def pieces(parts, lead, share, kind):
+    return [pltpu.VMEM((*lead, size // share, 16, 128), kind) for _, size in parts]
 
 
 def gather_call(own, targets, factor):
-    copies = 9 + 9 + 12 + 3 + 6 + 6 + 6
-    pts, held = factor.shape
-    wanted, tiles, steps = targets.shape[1], held // 128, pts // TILE_PTS
+    copies = 9 + 9 + 12 + 3 + 6 + 6 + 6 + 2 + 3 * 12
+    held, wanted = factor.shape[1], targets.shape[1]
+    tiles = held // 128
+    blocks = tiles * 8
     bf, f32, vmem = jnp.bfloat16, jnp.float32, pltpu.VMEM
-    out, cross, norms = pl.pallas_call(
+    scratch = [
+        vmem((wanted, held), f32),
+        vmem((2, blocks, 16, 128), bf),
+        vmem((tiles, 128), f32),
+        vmem((blocks, 16, 128), bf),
+        vmem((tiles, 128), f32),
+        vmem((blocks, 16, 128), f32),
+        vmem((blocks, 16, 128), bf),
+        vmem((4, tiles, 128), f32),
+        vmem((3, 3, tiles, 128), f32),
+    ]
+    scratch += pieces(HELD_PARTS, (3,), 4, bf) + pieces(HELD_PARTS, (3,), 16, bf)
+    scratch += pieces(HELD_PARTS, (3,), 16, bf) + pieces(HELD_PARTS, (), 4, f32)
+    scratch += pieces(HELD_PARTS, (), 4, bf) + pieces(HELD_PARTS, (), 16, bf)
+    steps = factor.shape[0] // TILE_PTS
+    scratch += [vmem((steps, TILE_PTS, held), bf), pltpu.SemaphoreType.DMA((steps,))]
+    scratch += [pltpu.SemaphoreType.DMA((copies,))] * 2
+    out, shard = pl.pallas_call(
         gather_kernel,
         out_shape=(
             jax.ShapeDtypeStruct((4, 2, 4, 4, *own.shape), bf),
-            jax.ShapeDtypeStruct((2, tiles * 8, 16, 128), bf),
-            jax.ShapeDtypeStruct((tiles, 128), f32),
+            jax.ShapeDtypeStruct((blocks // 16, 16, 128), bf),
         ),
         in_specs=[pl.BlockSpec(memory_space=vmem)] * 2 + [pl.BlockSpec(memory_space=pl.ANY)],
-        out_specs=[pl.BlockSpec(memory_space=vmem)] * 3,
-        scratch_shapes=[
-            vmem((steps, TILE_PTS, held), bf),
-            vmem((wanted, held), f32),
-            pltpu.SemaphoreType.DMA((copies,)),
-            pltpu.SemaphoreType.DMA((copies,)),
-            pltpu.SemaphoreType.DMA((steps,)),
-        ],
+        out_specs=[pl.BlockSpec(memory_space=vmem)] * 2,
+        scratch_shapes=scratch,
         compiler_params=pltpu.CompilerParams(
-            collective_id=2, has_side_effects=True, vmem_limit_bytes=48 << 20
+            collective_id=2, has_side_effects=True, vmem_limit_bytes=GATHER_VMEM
         ),
         name="gather_rows",
     )(own, targets, factor)
-    return out.reshape(128, *own.shape), cross, norms
+    return out.reshape(128, *own.shape), shard
 
 
 MICRO = 16
@@ -338,13 +459,7 @@
     ps_ref, pf_ref, sel_ref, a_ref, w_ref, lo_ref, hi_ref, down_hi, down_lo, fbuf, fsem,
 ):
     tiles = fbuf.shape[0]
-    copies = []
-    for i in range(tiles):
-        at = pl.ds(i * TILE_PTS, TILE_PTS)
-        copy = pltpu.make_async_copy(factor_ref.at[at, :], fbuf.at[i], fsem.at[i])
-        copy.start()
-        copies.append(copy)
-
+    loads = load_tiles(factor_ref, fbuf, fsem)
     padded = pos_ref.shape[1]
     sel_ref[...] = jnp.where(
         lax.broadcasted_iota(jnp.int32, (BLOCK, padded), 0) == pos_ref[...], 1.0, 0.0
@@ -373,8 +488,8 @@
     eye = lax.broadcasted_iota(jnp.int32, (PANEL, PANEL), 0) == lax.broadcasted_iota(
         jnp.int32, (PANEL, PANEL), 1
     )
-    for copy in copies:
-        copy.wait()
+    for load in loads:
+        load.wait()
 
     def exact(a, b):
         return jnp.dot(a, b, precision=HIGHEST, preferred_element_type=jnp.float32)
@@ -441,7 +556,6 @@
     features = points.shape[1]
     tiles = BLOCK // 128
     bf, f32, vmem = jnp.bfloat16, jnp.float32, pltpu.VMEM
-    steps = pts // TILE_PTS
     return pl.pallas_call(
         local_kernel,
         out_shape=(
@@ -461,195 +575,153 @@
             vmem((BLOCK, BLOCK), bf),
             vmem((BLOCK, pts), bf),
             vmem((BLOCK, pts), bf),
-            vmem((steps, TILE_PTS, held), bf),
-            pltpu.SemaphoreType.DMA((steps,)),
+            vmem((pts // TILE_PTS, TILE_PTS, held), bf),
+            pltpu.SemaphoreType.DMA((pts // TILE_PTS,)),
         ],
-        compiler_params=pltpu.CompilerParams(vmem_limit_bytes=44 << 20),
+        compiler_params=pltpu.CompilerParams(vmem_limit_bytes=LOCAL_VMEM),
         name="local_block",
     )(padded, positions, targets, points, factor)
 
 
 def sums_kernel(
-    xf_ref, xn_ref, nf_ref, nn_ref, out_ref, got0, sum0, out0, norm_got0, norm_sum, norm_got, coef, got_last,
-    a0, a1, a2, b0, b1, b2, c0, c1, c2, s1, s2, s3, t1, t2, t3, u1, u2, u3,
-    send, recv,
+    shard_ref, x_ref, n_ref, out_ref, coef, got_last, got0, norm_got0, sum0, out0, norm_sum,
+    norm_got, a0, a1, a2, b0, b1, b2, c0, c1, c2, u0, u1, u2, v0, v1, v2, send, recv,
 ):
     core, coords = place()
     partner = device_at(1 - core, coords)
     enter(core, coords)
-    count = [0]
-    sent = []
-
-    def start(src, dst, device):
-        k = count[0]
-        count[0] += 1
-        copy = pltpu.make_async_remote_copy(
-            src_ref=src, dst_ref=dst, send_sem=send.at[k], recv_sem=recv.at[k],
-            device_id=device, device_id_type=MESH,
-        )
-        copy.start()
-        sent.append(copy)
-        return copy
-
-    def arrive(copies):
-        for copy in copies:
-            copy.wait_recv()
-
-    wide = lambda v: v.astype(jnp.float32)
-    narrow = lambda v: v.astype(jnp.bfloat16)
-
-    split, tiles = xf_ref.shape[1], nf_ref.shape[0]
-    arrive([
-        start(xf_ref.at[1 - core], got0.at[:split], partner),
-        start(xn_ref.at[1 - core], got0.at[split:], partner),
-        start(nf_ref, norm_got0.at[:tiles], partner),
-        start(nn_ref, norm_got0.at[tiles : tiles + nn_ref.shape[0]], partner),
-    ])
-    for src, at in ((xf_ref, slice(0, split)), (xn_ref, slice(split, got0.shape[0]))):
-        value = wide(src[core]) + wide(got0[at])
-        sum0[at] = value
-        out0[at] = narrow(value)
-    last_tile = tiles + nn_ref.shape[0]
-    norm_sum[0, :tiles] = nf_ref[...] + norm_got0[:tiles]
-    norm_sum[0, tiles:last_tile] = nn_ref[...] + norm_got0[tiles:last_tile]
-    norm_sum[0, last_tile:] = jnp.zeros_like(norm_sum[0, last_tile:])
-
-    got = ((a0, a1, a2), (b0, b1, b2), (c0, c1, c2))
-    sums = ((s1, s2, s3), (t1, t2, t3))
-    outs = (u1, u2, u3)
-
-    copies, starts = [], []
-    for p, (order, base, size) in enumerate(PARTS):
-        here, quarter = coords[order[0]], size // 4
+    copies = Copies(send, recv)
+    split = coef.shape[0] - x_ref.shape[1]
+
+    def peer(axis, offset):
+        return device_at(core, coords, axis, offset)
+
+    zero = [
+        copies.start(x_ref.at[1 - core], got0, partner),
+        copies.start(n_ref, norm_got0, partner),
+    ]
+    held, at = [], 0
+    for order, (base, size) in zip(ORDERS, HELD_PARTS):
+        piece = size // 16
+        place_of = base + coords[order[0]] * (size // 4) + coords[order[1]] * piece
+        for o in range(1, 4):
+            held.append(
+                copies.start(
+                    shard_ref.at[at : at + piece], coef.at[pl.ds(place_of, piece)],
+                    peer(order[1], o),
+                )
+            )
+        coef[pl.ds(place_of, piece)] = shard_ref[at : at + piece]
+        at += piece
+
+    arrive(zero)
+    sum0[...] = wide(x_ref[core]) + wide(got0[...])
+    out0[...] = narrow(sum0[...])
+    norm_sum[0] = n_ref[...] + norm_got0[...]
+    one = []
+    for p, (order, (base, size)) in enumerate(zip(ORDERS, NEW_PARTS)):
+        here, piece = coords[order[0]], size // 4
         for o in range(1, 4):
             there = lax.rem(here + o, 4)
-            copies.append(
-                start(
-                    out0.at[pl.ds(base + there * quarter, quarter)],
-                    got[0][p].at[o - 1],
-                    device_at(core, coords, order[0], o),
-                )
-            )
-        starts.append(base + here * quarter)
-    for o in range(1, 4):
-        copies.append(
-            start(norm_sum.at[0], norm_got.at[0, o - 1], device_at(core, coords, 0, o))
-        )
-    arrive(copies)
-    for p, (order, base, size) in enumerate(PARTS):
-        quarter = size // 4
-        value = sum0[pl.ds(starts[p], quarter)]
-        for o in range(3):
-            value = value + wide(got[0][p][o])
-        sums[0][p][...] = value
-        outs[p][...] = narrow(value)
-    norm_sum[1] = norm_sum[0] + norm_got[0, 0] + norm_got[0, 1] + norm_got[0, 2]
-
-    copies = []
-    for p, (order, base, size) in enumerate(PARTS):
-        here, piece = coords[order[1]], size // 16
-        for o in range(1, 4):
-            there = lax.rem(here + o, 4)
-            copies.append(
-                start(
-                    outs[p].at[pl.ds(there * piece, piece)],
-                    got[1][p].at[o - 1],
-                    device_at(core, coords, order[1], o),
-                )
-            )
-        starts[p] = starts[p] + here * piece
-    for o in range(1, 4):
-        copies.append(
-            start(norm_sum.at[1], norm_got.at[1, o - 1], device_at(core, coords, 1, o))
-        )
-    arrive(copies)
-    for p, (order, base, size) in enumerate(PARTS):
-        here, piece = coords[order[1]], size // 16
-        value = sums[0][p][pl.ds(here * piece, piece)]
-        for o in range(3):
-            value = value + wide(got[1][p][o])
-        sums[1][p][0] = value
-        coef[pl.ds(starts[p], piece)] = narrow(value)
-    norm_sum[2] = norm_sum[1] + norm_got[1, 0] + norm_got[1, 1] + norm_got[1, 2]
-
-    copies = []
-    for p, (order, base, size) in enumerate(PARTS):
-        piece = size // 16
-        for o in range(1, 4):
-            copies.append(
-                start(
-                    coef.at[pl.ds(starts[p], piece)],
-                    got[2][p].at[o - 1],
-                    device_at(core, coords, order[2], o),
+            one.append(
+                copies.start(
+                    out0.at[pl.ds(base + there * piece, piece)],
+                    (a0, a1, a2)[p].at[o - 1],
+                    peer(order[0], o),
                 )
             )
     for o in range(1, 4):
-        copies.append(
-            start(norm_sum.at[2], norm_got.at[2, o - 1], device_at(core, coords, 2, o))
+        one.append(copies.start(norm_sum.at[0], norm_got.at[0, o - 1], peer(0, o)))
+
+    arrive(held)
+    held = []
+    for order, (base, size) in zip(ORDERS, HELD_PARTS):
+        block = coef.at[pl.ds(base + coords[order[0]] * (size // 4), size // 4)]
+        for o in range(1, 4):
+            held.append(copies.start(block, block, peer(order[0], o)))
+
+    values = []
+    arrive(one)
+    for p, (order, (base, size)) in enumerate(zip(ORDERS, NEW_PARTS)):
+        piece = size // 4
+        value = sum0[pl.ds(base + coords[order[0]] * piece, piece)]
+        for o in range(3):
+            value = value + wide((a0, a1, a2)[p][o])
+        values.append(value)
+    norm_sum[1] = norm_sum[0] + norm_got[0, 0] + norm_got[0, 1] + norm_got[0, 2]
+    last = []
+    for stage, sent, landed in ((1, (u0, u1, u2), (b0, b1, b2)), (2, (v0, v1, v2), (c0, c1, c2))):
+        line = []
+        for p, order in enumerate(ORDERS):
+            sent[p][...] = narrow(values[p])
+            for o in range(1, 4):
+                line.append(
+                    copies.start(sent[p], landed[p].at[o - 1], peer(order[stage], o))
+                )
+        for o in range(1, 4):
+            line.append(
+                copies.start(norm_sum.at[stage], norm_got.at[stage, o - 1], peer(stage, o))
+            )
+        if stage == 1:
+            arrive(held)
+            last.append(copies.start(coef.at[:split], got_last.at[:split], partner))
+        arrive(line)
+        for p in range(len(ORDERS)):
+            for o in range(3):
+                values[p] = values[p] + wide(landed[p][o])
+        norm_sum[stage + 1] = (
+            norm_sum[stage] + norm_got[stage, 0] + norm_got[stage, 1] + norm_got[stage, 2]
         )
-    arrive(copies)
-    for copy in copies:
-        copy.wait_send()
-    del sent[-len(copies):]
-    norm_sum[3] = norm_sum[2] + norm_got[2, 0] + norm_got[2, 1] + norm_got[2, 2]
-    for p, (order, base, size) in enumerate(PARTS):
-        piece = size // 16
-        value = sums[1][p][0]
-        for o in range(3):
-            value = value + wide(got[2][p][o])
+
+    back = []
+    for p, (order, (base, size)) in enumerate(zip(ORDERS, NEW_PARTS)):
+        piece = size // 4
+        start = base + coords[order[0]] * piece
         for i in range(piece):
-            tile = lax.div(starts[p] + i, 8)
-            norm = norm_sum[3, pl.ds(tile, 1), :]
-            coef[starts[p] + i] = narrow(value[i] / (norm + damping))
-
-    for stage, parts_of in ((1, 16), (0, 4)):
-        copies = []
-        for p, (order, base, size) in enumerate(PARTS):
-            piece = size // parts_of
-            if stage == 0:
-                starts[p] = base + coords[order[0]] * piece
-            block = coef.at[pl.ds(starts[p], piece)]
-            for o in range(1, 4):
-                copies.append(start(block, block, device_at(core, coords, order[stage], o)))
-        arrive(copies)
-    last = start(coef, got_last, partner)
-    out_ref[core] = coef[...]
-    last.wait_recv()
-    out_ref[1 - core] = got_last[...]
-    for copy in sent:
-        copy.wait_send()
-
-
-def sums_call(cross_f, cross_n, norms_f, norms_n):
-    blocks = cross_f.shape[1] + cross_n.shape[1]
-    tiles = 24
+            norm = norm_sum[3, pl.ds(lax.div(start + i, 8), 1), :]
+            coef[split + start + i] = narrow(values[p][i] / (norm + damping))
+        block = coef.at[pl.ds(split + start, piece)]
+        for o in range(1, 4):
+            back.append(copies.start(block, block, peer(order[0], o)))
+    out_ref[core, :split] = coef[:split]
+    last[0].wait_recv()
+    out_ref[1 - core, :split] = got_last[:split]
+    arrive(back)
+    last.append(copies.start(coef.at[split:], got_last.at[split:], partner))
+    out_ref[core, split:] = coef[split:]
+    last[1].wait_recv()
+    out_ref[1 - core, split:] = got_last[split:]
+    copies.finish()
+
+
+def sums_call(shard, cross, norms):
+    fresh, tiles = cross.shape[1], norms.shape[0]
+    blocks = shard.shape[0] * 16 + fresh
     bf, f32, vmem = jnp.bfloat16, jnp.float32, pltpu.VMEM
-    piece = lambda lead, n, kind: vmem((*lead, n, 16, 128), kind)
-    sizes = [size for _, _, size in PARTS]
     scratch = [
-        vmem((blocks, 16, 128), bf), vmem((blocks, 16, 128), f32), vmem((blocks, 16, 128), bf),
-        vmem((tiles, 128), f32), vmem((4, tiles, 128), f32), vmem((3, 3, tiles, 128), f32),
-        vmem((blocks, 16, 128), bf), vmem((blocks, 16, 128), bf),
+        vmem((blocks, 16, 128), bf),
+        vmem((blocks, 16, 128), bf),
+        vmem((fresh, 16, 128), bf),
+        vmem((tiles, 128), f32),
+        vmem((fresh, 16, 128), f32),
+        vmem((fresh, 16, 128), bf),
+        vmem((4, tiles, 128), f32),
+        vmem((3, 3, tiles, 128), f32),
     ]
-    scratch += [piece((3,), s // 4, bf) for s in sizes]
-    scratch += [piece((3,), s // 16, bf) for s in sizes]
-    scratch += [piece((3,), s // 16, bf) for s in sizes]
-    scratch += [piece((), s // 4, f32) for s in sizes]
-    scratch += [piece((1,), s // 16, f32) for s in sizes]
-    scratch += [piece((), s // 4, bf) for s in sizes]
-    copies = 4 + 12 * 3 + 9 * 2 + 1
+    scratch += pieces(NEW_PARTS, (3,), 4, bf) * 3 + pieces(NEW_PARTS, (), 4, bf) * 2
+    copies = 2 + 9 + 12 + 9 + 12 + 12 + 9 + 2
     scratch += [pltpu.SemaphoreType.DMA((copies,))] * 2
     return pl.pallas_call(
         sums_kernel,
         out_shape=jax.ShapeDtypeStruct((2, blocks, 16, 128), bf),
-        in_specs=[pl.BlockSpec(memory_space=vmem)] * 4,
+        in_specs=[pl.BlockSpec(memory_space=vmem)] * 3,
         out_specs=pl.BlockSpec(memory_space=vmem),
         scratch_shapes=scratch,
         compiler_params=pltpu.CompilerParams(
-            collective_id=1, has_side_effects=True, vmem_limit_bytes=24 << 20
+            collective_id=1, has_side_effects=True, vmem_limit_bytes=SUMS_VMEM
         ),
         name="sums",
-    )(cross_f, cross_n, norms_f, norms_n)
+    )(shard, cross, norms)
 
 
 def residual_kernel(factor_ref, new_ref, targets_ref, coef_ref, out_ref, turned_ref):
@@ -681,17 +753,17 @@
         ],
         out_specs=pl.BlockSpec((TILE_PTS, wanted), lambda i: (i, 0)),
         scratch_shapes=[pltpu.VMEM((wanted, held + BLOCK), jnp.bfloat16)],
-        compiler_params=pltpu.CompilerParams(vmem_limit_bytes=24 << 20),
+        compiler_params=pltpu.CompilerParams(vmem_limit_bytes=RESIDUAL_VMEM),
         name="residual",
     )(factor, new, targets, coef)
 
 
 def on_device(points, factor, targets, pivot_slots, pivot_counts):
     own = rows_call(pivot_slots, points, factor)
-    padded, cross_f, norms_f = gather_call(own, targets, factor)
+    padded, shard = gather_call(own, targets, factor)
     positions = padded_positions(pivot_counts, pivot_slots.shape[1])
-    new_columns, cross_n, norms_n = local_call(padded, positions, points, factor, targets)
-    coef = sums_call(cross_f, cross_n, norms_f, norms_n)
+    new_columns, cross, norms = local_call(padded, positions, points, factor, targets)
+    coef = sums_call(shard, cross, norms)
     residual_next = residual_call(factor, new_columns, targets, coef)
     return (new_columns, residual_next)
 

time: 102 us -> 95.4 us (0.935)
  Pallas kernels: 97.3 us -> 91.4 us
  local copies, waits for them, and re-layouts: 3.64 us -> 2.6 us
    pallas_call x1, Pallas kernels: 29.6 us -> 21.9 us  [sums_call(): pl.pallas_call(sums_kernel, out_shape=jax.ShapeDtypeStruct((2, blocks, 16...]
    pallas_call x1, Pallas kernels: 30.9 us -> 32.8 us  [gather_call(): pl.pallas_call(gather_kernel, out_shape=(jax.ShapeDtypeStruct((4, 2, 4, 4...]
    unnamed x16 -> x14, local copies, waits for them, and re-layouts: 3.43 us -> 2.38 us
where the time goes in v4:
time: 95.4 us; the launch traced here: 95.2 us
  Pallas kernels  91.4 us (96%)
  local copies, waits for them, and re-layouts  2.6 us (3%)
    pallas_call x1, Pallas kernels, gather_call(): pl.pallas_call(gather_kernel, out_shape=(jax.ShapeDtypeStruct((4, 2, 4, 4...  32.8 us
    pallas_call x1, Pallas kernels, local_call(): pl.pallas_call(local_kernel, out_shape=(jax.ShapeDtypeStruct((BLOCK, pts)...  29.4 us
    pallas_call x1, Pallas kernels, sums_call(): pl.pallas_call(sums_kernel, out_shape=jax.ShapeDtypeStruct((2, blocks, 16...  21.9 us
    pallas_call x1, Pallas kernels, residual_call(): pl.pallas_call(residual_kernel, grid=(pts // TILE_PTS,), out_shape=jax.Sh...  4.64 us
    pallas_call x1, Pallas kernels, rows_call(): pl.pallas_call(rows_kernel, out_shape=jax.ShapeDtypeStruct(((features + h...  2.73 us
    unnamed x14, local copies, waits for them, and re-layouts  2.38 us

profile of v4, /device:TPU:1, one launch (start us, length us, event | category | flops | bytes accessed | tf_op | source)
XLA Modules:
  0.0 95.2 jit_solution(7492575008974642987)
XLA Ops:
  0.6 0.0 copy-start.4
  0.6 0.0 copy-start
  0.7 2.7 %pivot_rows.1.own_ref = bf16[20,8,128]{2,1,0:T(8,128)(2,1)} custom-call(s32[1,8]{1,0:T(1,128)} %slots_ref.1, bf16[2048,512]{1,0:T(8,128)(2,1)} %points_ref.3, bf16[2048,2048]{1,0:T(8,128)(2,1)} %factor_ref.7), custom_call_target="tpu_custom_call" | custom-call | tf_op jit(solution)/shard_map/pivot_rows/pallas_call | solution.py:158
  3.4 0.0 copy-done.4
  3.4 0.1 copy.8
  3.5 0.2 reduce-window.9
  3.7 0.1 reduce
  3.8 0.1 add_select_fusion
  3.9 0.1 select_n.15.pos_ref
  4.0 0.0 copy-done
  4.0 0.0 copy-start.3
  4.0 0.8 copy-done.3
  4.8 0.0 copy-start.1
  4.8 32.8 %gather_rows.1 = (bf16[4,2,4,4,20,8,128]{6,5,4,3,2,1,0:T(8,128)(2,1)S(1)}, bf16[8,16,128]{2,1,0:T(8,128)(2,1)S(1)}) custom-call(bf16[20,8,128]{2,1,0:T(8,128)(2,1)S(1)} %copy-done.3, bf16[2048,256]{1,0:T(8,128)(2,1)S(1)} %copy-done, bf16[2048,2048]{1,0:T(8,128)(2,1)} %factor_ref.7), custom_call_target="tpu_custom_call" | custom-call | tf_op jit(solution)/shard_map/gather_rows/pallas_call | solution.py:375
  37.6 0.0 slice-start
  37.6 0.0 copy-done.1
  37.6 0.0 slice-start.1
  37.6 29.4 %local_block.1 = (bf16[512,2048]{1,0:T(8,128)(2,1)}, bf16[2,32,16,128]{3,2,1,0:T(8,128)(2,1)S(1)}, f32[4,128]{1,0:T(4,128)S(1)}) custom-call(bf16[128,20,8,128]{3,2,1,0:T(8,128)(2,1)S(1)} %bitcast.4, s32[1,1024]{1,0:T(1,128)S(1)} %select_n.15.pos_ref, bf16[2048,256]{1,0:T(8,128)(2,1)S(1)} %copy-done, bf16[2048,512]{1,0:T(8,128)(2,1)S(1)} %copy-done.1, ...), custom_call_target="tpu_custom_call" | custom-call | tf_op jit(solution)/shard_map/local_block/pallas_call | solution.py:559
  67.1 21.9 %sums.1.coef_ref = bf16[2,160,16,128]{3,2,1,0:T(8,128)(2,1)S(1)} custom-call(bf16[8,16,128]{2,1,0:T(8,128)(2,1)S(1)} %get-tuple-element.9.shard_ref, bf16[2,32,16,128]{3,2,1,0:T(8,128)(2,1)S(1)} %get-tuple-element.10.x_ref, f32[4,128]{1,0:T(4,128)S(1)} %get-tuple-element.11.n_ref), custom_call_target="tpu_custom_call" | custom-call | tf_op jit(solution)/shard_map/sums/pallas_call | solution.py:714
  88.9 0.0 slice-done
  88.9 0.0 slice-done.1
  88.9 0.0 copy-start.2
  88.9 1.6 %copy-done.2 = bf16[512,2048]{1,0:T(8,128)(2,1)S(1)} copy-done((bf16[512,2048]{1,0:T(8,128)(2,1)S(1)}, bf16[512,2048]{1,0:T(8,128)(2,1)}, u32[]{:S(2)}) %copy-start.2) | copy-done | bytes 2097176
  90.5 4.6 %residual.1 = f32[2048,256]{1,0:T(8,128)} custom-call(bf16[2048,2048]{1,0:T(8,128)(2,1)S(1)} %bitcast.3, bf16[512,2048]{1,0:T(8,128)(2,1)S(1)} %copy-done.2, bf16[2048,256]{1,0:T(8,128)(2,1)S(1)} %copy-done, bf16[2,160,16,128]{3,2,1,0:T(8,128)(2,1)S(1)} %sums.1.coef_ref), custom_call_target="tpu_custom_call" | custom-call | tf_op jit(solution)/shard_map/residual/pallas_call | solution.py:744
  (2 shorter events, 0.0 us)
Async XLA Ops:
  0.6 2.8 %copy-start.4 = (s32[128]{0:T(128)S(1)}, s32[128]{0:T(128)}, u32[]{:S(2)}) copy-start(s32[128]{0:T(128)} %param.9) | copy-start | bytes 1540
  0.6 3.4 %copy-start = (bf16[2048,256]{1,0:T(8,128)(2,1)S(1)}, bf16[2048,256]{1,0:T(8,128)(2,1)}, u32[]{:S(2)}) copy-start(bf16[2048,256]{1,0:T(8,128)(2,1)} %targets_ref.5) | copy-start | bytes 3145732
  4.0 0.8 copy-start.3
  4.8 32.8 %copy-start.1 = (bf16[2048,512]{1,0:T(8,128)(2,1)S(1)}, bf16[2048,512]{1,0:T(8,128)(2,1)}, u32[]{:S(2)}) copy-start(bf16[2048,512]{1,0:T(8,128)(2,1)} %points_ref.3) | copy-start | bytes 6291460
  37.6 51.3 %slice-start = ((s8[8388608]{0:T(1024)(128)(4,1)}), s8[4194304]{0:T(1024)(128)(4,1)S(1)}, s32[]{:S(2)}) async-start(s8[8388608]{0:T(1024)(128)(4,1)} %bitcast.2), calls=%async_computation | async-start | bytes 8388608
  37.6 51.3 %slice-start.1 = ((s8[8388608]{0:T(1024)(128)(4,1)}), s8[4194304]{0:T(1024)(128)(4,1)S(1)}, s32[]{:S(2)}) async-start(s8[8388608]{0:T(1024)(128)(4,1)} %bitcast.2), calls=%async_computation.1 | async-start | bytes 8388608
  88.9 1.6 %copy-start.2 = (bf16[512,2048]{1,0:T(8,128)(2,1)S(1)}, bf16[512,2048]{1,0:T(8,128)(2,1)}, u32[]{:S(2)}) copy-start(bf16[512,2048]{1,0:T(8,128)(2,1)} %get-tuple-element.5.new_ref) | copy-start | bytes 6291460

commit v5 on v4

--- a/solution.py
+++ b/solution.py
@@ -12,7 +12,7 @@
 SUB = 8
 TILE_PTS = 512
 ROWS_VMEM, GATHER_VMEM, LOCAL_VMEM, SUMS_VMEM, RESIDUAL_VMEM = (
-    mib << 20 for mib in (60, 40, 38, 16, 16)
+    mib << 20 for mib in (62, 40, 38, 20, 16)
 )
 MESH = pl.DeviceIdType.MESH
 HIGHEST = lax.Precision.HIGHEST
@@ -584,7 +584,7 @@
 
 
 def sums_kernel(
-    shard_ref, x_ref, n_ref, out_ref, coef, got_last, got0, norm_got0, sum0, out0, norm_sum,
+    shard_ref, x_ref, n_ref, factor_ref, out_ref, fit_ref, turned_ref, coef, got_last, got0, norm_got0, sum0, out0, norm_sum,
     norm_got, a0, a1, a2, b0, b1, b2, c0, c1, c2, u0, u1, u2, v0, v1, v2, send, recv,
 ):
     core, coords = place()
@@ -592,6 +592,7 @@
     enter(core, coords)
     copies = Copies(send, recv)
     split = coef.shape[0] - x_ref.shape[1]
+    tiles = factor_ref.shape[0] // TILE_PTS
 
     def peer(axis, offset):
         return device_at(core, coords, axis, offset)
@@ -613,6 +614,11 @@
             )
         coef[pl.ds(place_of, piece)] = shard_ref[at : at + piece]
         at += piece
+
+    def fit(tiles):
+        for i in tiles:
+            at = slice(i * TILE_PTS, (i + 1) * TILE_PTS)
+            fit_ref[at, :] = dot_nt(factor_ref[at, :], turned_ref[...])
 
     arrive(zero)
     sum0[...] = wide(x_ref[core]) + wide(got0[...])
@@ -665,6 +671,15 @@
         if stage == 1:
             arrive(held)
             last.append(copies.start(coef.at[:split], got_last.at[:split], partner))
+        else:
+            last[0].wait_recv()
+            rows = turned_ref.shape[0] // 2
+            for t in range(split // 8):
+                lanes = slice(t * 128, (t + 1) * 128)
+                for half, blocks in ((core, coef), (1 - core, got_last)):
+                    at = pl.ds(pl.multiple_of(half * rows, rows), rows)
+                    turned_ref[at, lanes] = blocks[t * 8 : (t + 1) * 8].reshape(rows, 128)
+            fit(range(tiles // 2))
         arrive(line)
         for p in range(len(ORDERS)):
             for o in range(3):
@@ -683,22 +698,22 @@
         block = coef.at[pl.ds(split + start, piece)]
         for o in range(1, 4):
             back.append(copies.start(block, block, peer(order[0], o)))
-    out_ref[core, :split] = coef[:split]
-    last[0].wait_recv()
-    out_ref[1 - core, :split] = got_last[:split]
+    fit(range(tiles // 2, tiles))
     arrive(back)
     last.append(copies.start(coef.at[split:], got_last.at[split:], partner))
-    out_ref[core, split:] = coef[split:]
+    out_ref[core] = coef[split:]
     last[1].wait_recv()
-    out_ref[1 - core, split:] = got_last[split:]
+    out_ref[1 - core] = got_last[split:]
     copies.finish()
 
 
-def sums_call(shard, cross, norms):
+def sums_call(shard, cross, norms, factor, wanted):
     fresh, tiles = cross.shape[1], norms.shape[0]
     blocks = shard.shape[0] * 16 + fresh
     bf, f32, vmem = jnp.bfloat16, jnp.float32, pltpu.VMEM
+    pts, held = factor.shape
     scratch = [
+        vmem((wanted, held), bf),
         vmem((blocks, 16, 128), bf),
         vmem((blocks, 16, 128), bf),
         vmem((fresh, 16, 128), bf),
@@ -713,49 +728,48 @@
     scratch += [pltpu.SemaphoreType.DMA((copies,))] * 2
     return pl.pallas_call(
         sums_kernel,
-        out_shape=jax.ShapeDtypeStruct((2, blocks, 16, 128), bf),
-        in_specs=[pl.BlockSpec(memory_space=vmem)] * 3,
-        out_specs=pl.BlockSpec(memory_space=vmem),
+        out_shape=(
+            jax.ShapeDtypeStruct((2, fresh, 16, 128), bf),
+            jax.ShapeDtypeStruct((pts, wanted), f32),
+        ),
+        in_specs=[pl.BlockSpec(memory_space=vmem)] * 4,
+        out_specs=[pl.BlockSpec(memory_space=vmem)] * 2,
         scratch_shapes=scratch,
         compiler_params=pltpu.CompilerParams(
             collective_id=1, has_side_effects=True, vmem_limit_bytes=SUMS_VMEM
         ),
         name="sums",
-    )(shard, cross, norms)
-
-
-def residual_kernel(factor_ref, new_ref, targets_ref, coef_ref, out_ref, turned_ref):
-    held = factor_ref.shape[1]
-
-    @pl.when(pl.program_id(0) == 0)
-    def _():
-        for t in range(turned_ref.shape[1] // 128):
-            lanes = slice(t * 128, (t + 1) * 128)
-            turned_ref[:, lanes] = coef_ref[:, t * 8 : (t + 1) * 8].reshape(-1, 128)
-
-    fitted = dot_nt(factor_ref[...], turned_ref[:, :held])
-    fitted = fitted + dot_nn(turned_ref[:, held:], new_ref[...]).T
-    out_ref[...] = targets_ref[...].astype(jnp.float32) - fitted
-
-
-def residual_call(factor, new, targets, coef):
-    pts, held = factor.shape
-    wanted = targets.shape[1]
+    )(shard, cross, norms, factor)
+
+
+def residual_kernel(new_ref, targets_ref, fit_ref, coef_ref, out_ref):
+    turned = jnp.concatenate(
+        [
+            coef_ref[:, t * 8 : (t + 1) * 8].reshape(-1, 128)
+            for t in range(coef_ref.shape[1] // 8)
+        ],
+        axis=1,
+    )
+    fitted = fit_ref[...] + dot_nn(turned, new_ref[...]).T
+    out_ref[...] = wide(targets_ref[...]) - fitted
+
+
+def residual_call(new, targets, fit, coef):
+    pts, wanted = targets.shape
     return pl.pallas_call(
         residual_kernel,
         grid=(pts // TILE_PTS,),
         out_shape=jax.ShapeDtypeStruct((pts, wanted), jnp.float32),
         in_specs=[
-            pl.BlockSpec((TILE_PTS, held), lambda i: (i, 0)),
             pl.BlockSpec((BLOCK, TILE_PTS), lambda i: (0, i)),
+            pl.BlockSpec((TILE_PTS, wanted), lambda i: (i, 0)),
             pl.BlockSpec((TILE_PTS, wanted), lambda i: (i, 0)),
             pl.BlockSpec(coef.shape, lambda i: (0, 0, 0, 0), pipeline_mode=pl.Buffered(1)),
         ],
         out_specs=pl.BlockSpec((TILE_PTS, wanted), lambda i: (i, 0)),
-        scratch_shapes=[pltpu.VMEM((wanted, held + BLOCK), jnp.bfloat16)],
         compiler_params=pltpu.CompilerParams(vmem_limit_bytes=RESIDUAL_VMEM),
         name="residual",
-    )(factor, new, targets, coef)
+    )(new, targets, fit, coef)
 
 
 def on_device(points, factor, targets, pivot_slots, pivot_counts):
@@ -763,8 +777,8 @@
     padded, shard = gather_call(own, targets, factor)
     positions = padded_positions(pivot_counts, pivot_slots.shape[1])
     new_columns, cross, norms = local_call(padded, positions, points, factor, targets)
-    coef = sums_call(shard, cross, norms)
-    residual_next = residual_call(factor, new_columns, targets, coef)
+    coef, fit = sums_call(shard, cross, norms, factor, targets.shape[1])
+    residual_next = residual_call(new_columns, targets, fit, coef)
     return (new_columns, residual_next)
 
 

time: 95.4 us -> 92.3 us (0.968)
  Pallas kernels: 91.4 us -> 89.8 us
  local copies, waits for them, and re-layouts: 2.6 us -> 1.02 us
    unnamed x14, local copies, waits for them, and re-layouts: 2.38 us -> 0.8 us
    pallas_call x1, Pallas kernels: 4.64 us -> 3.07 us  [residual_call(): pl.pallas_call(residual_kernel, grid=(pts // TILE_PTS,), out_shape=jax.Sh...]
where the time goes in v5:
time: 92.3 us; the launch traced here: 92 us
  Pallas kernels  89.8 us (97%)
  local copies, waits for them, and re-layouts  1.02 us (1%)
    pallas_call x1, Pallas kernels, gather_call(): pl.pallas_call(gather_kernel, out_shape=(jax.ShapeDtypeStruct((4, 2, 4, 4...  32.8 us
    pallas_call x1, Pallas kernels, local_call(): pl.pallas_call(local_kernel, out_shape=(jax.ShapeDtypeStruct((BLOCK, pts)...  29.4 us
    pallas_call x1, Pallas kernels, sums_call(): pl.pallas_call(sums_kernel, out_shape=(jax.ShapeDtypeStruct((2, fresh, 16...  21.9 us
    pallas_call x1, Pallas kernels, residual_call(): pl.pallas_call(residual_kernel, grid=(pts // TILE_PTS,), out_shape=jax.Sh...  3.07 us
    pallas_call x1, Pallas kernels, rows_call(): pl.pallas_call(rows_kernel, out_shape=jax.ShapeDtypeStruct(((features + h...  2.73 us

profile of v5, /device:TPU:1, one launch (start us, length us, event | category | flops | bytes accessed | tf_op | source)
XLA Modules:
  0.0 92.0 jit_solution(13358897252041176669)
XLA Ops:
  0.6 0.0 copy-start.4
  0.6 0.0 copy-start
  0.7 2.7 %pivot_rows.1.own_ref = bf16[20,8,128]{2,1,0:T(8,128)(2,1)} custom-call(s32[1,8]{1,0:T(1,128)} %slots_ref.1, bf16[2048,512]{1,0:T(8,128)(2,1)} %points_ref.3, bf16[2048,2048]{1,0:T(8,128)(2,1)} %factor_ref.7), custom_call_target="tpu_custom_call" | custom-call | tf_op jit(solution)/shard_map/pivot_rows/pallas_call | solution.py:158
  3.4 0.0 copy-done.4
  3.4 0.1 copy.8
  3.5 0.2 reduce-window.9
  3.7 0.1 reduce
  3.8 0.1 add_select_fusion
  3.9 0.1 select_n.15.pos_ref
  4.0 0.0 copy-done
  4.0 0.0 copy-start.3
  4.0 0.8 copy-done.3
  4.8 0.0 copy-start.1
  4.8 32.8 %gather_rows.1 = (bf16[4,2,4,4,20,8,128]{6,5,4,3,2,1,0:T(8,128)(2,1)S(1)}, bf16[8,16,128]{2,1,0:T(8,128)(2,1)S(1)}) custom-call(bf16[20,8,128]{2,1,0:T(8,128)(2,1)S(1)} %copy-done.3, bf16[2048,256]{1,0:T(8,128)(2,1)S(1)} %copy-done, bf16[2048,2048]{1,0:T(8,128)(2,1)} %factor_ref.7), custom_call_target="tpu_custom_call" | custom-call | tf_op jit(solution)/shard_map/gather_rows/pallas_call | solution.py:375
  37.6 0.0 slice-start
  37.6 0.0 copy-done.1
  37.6 0.0 slice-start.1
  37.6 29.4 %local_block.1 = (bf16[512,2048]{1,0:T(8,128)(2,1)}, bf16[2,32,16,128]{3,2,1,0:T(8,128)(2,1)S(1)}, f32[4,128]{1,0:T(4,128)S(1)}) custom-call(bf16[128,20,8,128]{3,2,1,0:T(8,128)(2,1)S(1)} %bitcast.4, s32[1,1024]{1,0:T(1,128)S(1)} %select_n.15.pos_ref, bf16[2048,256]{1,0:T(8,128)(2,1)S(1)} %copy-done, bf16[2048,512]{1,0:T(8,128)(2,1)S(1)} %copy-done.1, ...), custom_call_target="tpu_custom_call" | custom-call | tf_op jit(solution)/shard_map/local_block/pallas_call | solution.py:559
  67.1 0.0 slice-done
  67.1 0.0 slice-done.1
  67.1 0.0 copy-start.2
  67.1 21.9 %sums.1 = (bf16[2,32,16,128]{3,2,1,0:T(8,128)(2,1)S(1)}, f32[2048,256]{1,0:T(8,128)S(1)}) custom-call(bf16[8,16,128]{2,1,0:T(8,128)(2,1)S(1)} %get-tuple-element.11.shard_ref, bf16[2,32,16,128]{3,2,1,0:T(8,128)(2,1)S(1)} %get-tuple-element.12.x_ref, f32[4,128]{1,0:T(4,128)S(1)} %get-tuple-element.13.n_ref, bf16[2048,2048]{1,0:T(8,128)(2,1)S(1)} %bitcast.3), custom_call_target="tpu_custom_call" | custom-call | tf_op jit(solution)/shard_map/sums/pallas_call | solution.py:729
  89.0 0.0 copy-done.2
  89.0 3.1 %residual.1 = f32[2048,256]{1,0:T(8,128)} custom-call(bf16[512,2048]{1,0:T(8,128)(2,1)S(1)} %copy-done.2, bf16[2048,256]{1,0:T(8,128)(2,1)S(1)} %copy-done, f32[2048,256]{1,0:T(8,128)S(1)} %get-tuple-element.14.fit_ref, bf16[2,32,16,128]{3,2,1,0:T(8,128)(2,1)S(1)} %get-tuple-element.15.coef_ref), custom_call_target="tpu_custom_call" | custom-call | tf_op jit(solution)/shard_map/residual/pallas_call | solution.py:759
  (2 shorter events, 0.0 us)
Async XLA Ops:
  0.6 2.8 %copy-start.4 = (s32[128]{0:T(128)S(1)}, s32[128]{0:T(128)}, u32[]{:S(2)}) copy-start(s32[128]{0:T(128)} %param.9) | copy-start | bytes 1540
  0.6 3.4 %copy-start = (bf16[2048,256]{1,0:T(8,128)(2,1)S(1)}, bf16[2048,256]{1,0:T(8,128)(2,1)}, u32[]{:S(2)}) copy-start(bf16[2048,256]{1,0:T(8,128)(2,1)} %targets_ref.5) | copy-start | bytes 3145732
  4.0 0.8 copy-start.3
  4.8 32.8 %copy-start.1 = (bf16[2048,512]{1,0:T(8,128)(2,1)S(1)}, bf16[2048,512]{1,0:T(8,128)(2,1)}, u32[]{:S(2)}) copy-start(bf16[2048,512]{1,0:T(8,128)(2,1)} %points_ref.3) | copy-start | bytes 6291460
  37.6 29.5 %slice-start = ((s8[8388608]{0:T(1024)(128)(4,1)}), s8[4194304]{0:T(1024)(128)(4,1)S(1)}, s32[]{:S(2)}) async-start(s8[8388608]{0:T(1024)(128)(4,1)} %bitcast.2), calls=%async_computation | async-start | bytes 8388608
  37.6 29.4 %slice-start.1 = ((s8[8388608]{0:T(1024)(128)(4,1)}), s8[4194304]{0:T(1024)(128)(4,1)S(1)}, s32[]{:S(2)}) async-start(s8[8388608]{0:T(1024)(128)(4,1)} %bitcast.2), calls=%async_computation.1 | async-start | bytes 8388608
  67.1 21.9 %copy-start.2 = (bf16[512,2048]{1,0:T(8,128)(2,1)S(1)}, bf16[512,2048]{1,0:T(8,128)(2,1)}, u32[]{:S(2)}) copy-start(bf16[512,2048]{1,0:T(8,128)(2,1)} %get-tuple-element.7.new_ref) | copy-start | bytes 6291460

commit v6 on v5

--- a/solution.py
+++ b/solution.py
@@ -234,18 +234,6 @@
         copies.start(x_ref.at[1 - core], got0, partner),
         copies.start(n_ref, norm_got0, partner),
     ]
-    third, across = [], []
-    for p, (order, (low, mid, high)) in enumerate(zip(ORDERS, SPANS)):
-        arrive(second[p])
-        left, right = peer(order[2], 3), peer(order[2], 1)
-        halves = [region(a, b, order[:2]) for a, b in ((low, mid), (mid, high))]
-        right_low = push(halves[0], right)
-        left_high = push(halves[1], left)
-        right_high = push(halves[1], right)
-        left_low = push(halves[0], left)
-        third.append((right_low, left_high, right_high, left_low))
-        across.append(push(region(low, high, order[:2]), partner))
-
     arrive(zero)
     sum0[...] = wide(x_ref[core]) + wide(got0[...])
     out0[...] = narrow(sum0[...])
@@ -265,6 +253,18 @@
         starts.append(base + here * piece)
     for o in range(1, 4):
         one.append(copies.start(norm_sum.at[0], norm_got.at[0, o - 1], peer(0, o)))
+
+    third, across = [], []
+    for p, (order, (low, mid, high)) in enumerate(zip(ORDERS, SPANS)):
+        arrive(second[p])
+        left, right = peer(order[2], 3), peer(order[2], 1)
+        halves = [region(a, b, order[:2]) for a, b in ((low, mid), (mid, high))]
+        right_low = push(halves[0], right)
+        left_high = push(halves[1], left)
+        right_high = push(halves[1], right)
+        left_low = push(halves[0], left)
+        third.append((right_low, left_high, right_high, left_low))
+        across.append(push(region(low, high, order[:2]), partner))
 
     relays = []
     for p, (order, (low, mid, high)) in enumerate(zip(ORDERS, SPANS)):

time: 92.3 us -> 91.7 us (level)
  no operation moved by 1% of the time
where the time goes in v6:
time: 91.7 us; the launch traced here: 91.5 us
  Pallas kernels  89.3 us (97%)
  local copies, waits for them, and re-layouts  1.02 us (1%)
    pallas_call x1, Pallas kernels, gather_call(): pl.pallas_call(gather_kernel, out_shape=(jax.ShapeDtypeStruct((4, 2, 4, 4...  32.9 us
    pallas_call x1, Pallas kernels, local_call(): pl.pallas_call(local_kernel, out_shape=(jax.ShapeDtypeStruct((BLOCK, pts)...  29.4 us
    pallas_call x1, Pallas kernels, sums_call(): pl.pallas_call(sums_kernel, out_shape=(jax.ShapeDtypeStruct((2, fresh, 16...  21.1 us
    pallas_call x1, Pallas kernels, residual_call(): pl.pallas_call(residual_kernel, grid=(pts // TILE_PTS,), out_shape=jax.Sh...  3.06 us
    pallas_call x1, Pallas kernels, rows_call(): pl.pallas_call(rows_kernel, out_shape=jax.ShapeDtypeStruct(((features + h...  2.73 us

profile of v6, /device:TPU:1, one launch (start us, length us, event | category | flops | bytes accessed | tf_op | source)
XLA Modules:
  0.0 91.5 jit_solution(5222041473008137900)
XLA Ops:
  0.6 0.0 copy-start.4
  0.6 0.0 copy-start
  0.7 2.7 %pivot_rows.1.own_ref = bf16[20,8,128]{2,1,0:T(8,128)(2,1)} custom-call(s32[1,8]{1,0:T(1,128)} %slots_ref.1, bf16[2048,512]{1,0:T(8,128)(2,1)} %points_ref.3, bf16[2048,2048]{1,0:T(8,128)(2,1)} %factor_ref.7), custom_call_target="tpu_custom_call" | custom-call | tf_op jit(solution)/shard_map/pivot_rows/pallas_call | solution.py:158
  3.4 0.0 copy-done.4
  3.4 0.1 copy.8
  3.5 0.2 reduce-window.9
  3.7 0.1 reduce
  3.8 0.1 add_select_fusion
  3.9 0.1 select_n.15.pos_ref
  4.0 0.0 copy-done
  4.0 0.0 copy-start.3
  4.0 0.8 copy-done.3
  4.8 0.0 copy-start.1
  4.8 32.9 %gather_rows.1 = (bf16[4,2,4,4,20,8,128]{6,5,4,3,2,1,0:T(8,128)(2,1)S(1)}, bf16[8,16,128]{2,1,0:T(8,128)(2,1)S(1)}) custom-call(bf16[20,8,128]{2,1,0:T(8,128)(2,1)S(1)} %copy-done.3, bf16[2048,256]{1,0:T(8,128)(2,1)S(1)} %copy-done, bf16[2048,2048]{1,0:T(8,128)(2,1)} %factor_ref.7), custom_call_target="tpu_custom_call" | custom-call | tf_op jit(solution)/shard_map/gather_rows/pallas_call | solution.py:375
  37.8 0.0 slice-start
  37.8 0.0 copy-done.1
  37.8 0.0 slice-start.1
  37.8 29.4 %local_block.1 = (bf16[512,2048]{1,0:T(8,128)(2,1)}, bf16[2,32,16,128]{3,2,1,0:T(8,128)(2,1)S(1)}, f32[4,128]{1,0:T(4,128)S(1)}) custom-call(bf16[128,20,8,128]{3,2,1,0:T(8,128)(2,1)S(1)} %bitcast.4, s32[1,1024]{1,0:T(1,128)S(1)} %select_n.15.pos_ref, bf16[2048,256]{1,0:T(8,128)(2,1)S(1)} %copy-done, bf16[2048,512]{1,0:T(8,128)(2,1)S(1)} %copy-done.1, ...), custom_call_target="tpu_custom_call" | custom-call | tf_op jit(solution)/shard_map/local_block/pallas_call | solution.py:559
  67.2 0.0 slice-done
  67.2 0.0 slice-done.1
  67.2 0.0 copy-start.2
  67.3 21.1 %sums.1 = (bf16[2,32,16,128]{3,2,1,0:T(8,128)(2,1)S(1)}, f32[2048,256]{1,0:T(8,128)S(1)}) custom-call(bf16[8,16,128]{2,1,0:T(8,128)(2,1)S(1)} %get-tuple-element.11.shard_ref, bf16[2,32,16,128]{3,2,1,0:T(8,128)(2,1)S(1)} %get-tuple-element.12.x_ref, f32[4,128]{1,0:T(4,128)S(1)} %get-tuple-element.13.n_ref, bf16[2048,2048]{1,0:T(8,128)(2,1)S(1)} %bitcast.3), custom_call_target="tpu_custom_call" | custom-call | tf_op jit(solution)/shard_map/sums/pallas_call | solution.py:729
  88.4 0.0 copy-done.2
  88.4 3.1 %residual.1 = f32[2048,256]{1,0:T(8,128)} custom-call(bf16[512,2048]{1,0:T(8,128)(2,1)S(1)} %copy-done.2, bf16[2048,256]{1,0:T(8,128)(2,1)S(1)} %copy-done, f32[2048,256]{1,0:T(8,128)S(1)} %get-tuple-element.14.fit_ref, bf16[2,32,16,128]{3,2,1,0:T(8,128)(2,1)S(1)} %get-tuple-element.15.coef_ref), custom_call_target="tpu_custom_call" | custom-call | tf_op jit(solution)/shard_map/residual/pallas_call | solution.py:759
  (2 shorter events, 0.0 us)
Async XLA Ops:
  0.6 2.8 %copy-start.4 = (s32[128]{0:T(128)S(1)}, s32[128]{0:T(128)}, u32[]{:S(2)}) copy-start(s32[128]{0:T(128)} %param.9) | copy-start | bytes 1540
  0.6 3.4 %copy-start = (bf16[2048,256]{1,0:T(8,128)(2,1)S(1)}, bf16[2048,256]{1,0:T(8,128)(2,1)}, u32[]{:S(2)}) copy-start(bf16[2048,256]{1,0:T(8,128)(2,1)} %targets_ref.5) | copy-start | bytes 3145732
  4.0 0.8 copy-start.3
  4.8 33.0 %copy-start.1 = (bf16[2048,512]{1,0:T(8,128)(2,1)S(1)}, bf16[2048,512]{1,0:T(8,128)(2,1)}, u32[]{:S(2)}) copy-start(bf16[2048,512]{1,0:T(8,128)(2,1)} %points_ref.3) | copy-start | bytes 6291460
  37.8 29.5 %slice-start = ((s8[8388608]{0:T(1024)(128)(4,1)}), s8[4194304]{0:T(1024)(128)(4,1)S(1)}, s32[]{:S(2)}) async-start(s8[8388608]{0:T(1024)(128)(4,1)} %bitcast.2), calls=%async_computation | async-start | bytes 8388608
  37.8 29.4 %slice-start.1 = ((s8[8388608]{0:T(1024)(128)(4,1)}), s8[4194304]{0:T(1024)(128)(4,1)S(1)}, s32[]{:S(2)}) async-start(s8[8388608]{0:T(1024)(128)(4,1)} %bitcast.2), calls=%async_computation.1 | async-start | bytes 8388608
  67.2 21.1 %copy-start.2 = (bf16[512,2048]{1,0:T(8,128)(2,1)S(1)}, bf16[512,2048]{1,0:T(8,128)(2,1)}, u32[]{:S(2)}) copy-start(bf16[512,2048]{1,0:T(8,128)(2,1)} %get-tuple-element.7.new_ref) | copy-start | bytes 6291460

commit v7 on v6

--- a/solution.py
+++ b/solution.py
@@ -28,13 +28,6 @@
     return (values * factor_scale).astype(jnp.bfloat16)
 
 
-def padded_positions(pivot_counts, slot_cap):
-    starts = jnp.cumsum(pivot_counts) - pivot_counts
-    slot = jnp.arange(slot_cap, dtype=jnp.int32)[None, :]
-    place_of = jnp.where(slot < pivot_counts[:, None], starts[:, None] + slot, -1)
-    return place_of.astype(jnp.int32).reshape(1, -1)
-
-
 def dot_nt(a, b):
     return lax.dot_general(a, b, (((1,), (1,)), ((), ())), preferred_element_type=jnp.float32)
 
@@ -121,7 +114,9 @@
     return value.astype(jnp.bfloat16)
 
 
-def rows_kernel(slots_ref, points_ref, factor_ref, out_ref, pbuf, fbuf, psem, fsem):
+def rows_kernel(
+    slots_ref, counts_ref, points_ref, factor_ref, out_ref, pos_ref, pbuf, fbuf, psem, fsem
+):
     cap = pbuf.shape[0]
     copies = []
     for s in range(cap):
@@ -130,6 +125,21 @@
             copy = pltpu.make_async_copy(src.at[pl.ds(base, SUB), :], buf.at[s], sem.at[s])
             copy.start()
             copies.append(copy)
+
+    owners, padded = counts_ref.shape[1], pos_ref.shape[1]
+    first = cap * lax.broadcasted_iota(jnp.int32, (owners, padded), 0)
+    row = lax.broadcasted_iota(jnp.int32, (owners, padded), 1)
+    counts = jnp.broadcast_to(wide(counts_ref[...]), (SUB, owners)).astype(jnp.bfloat16)
+
+    def total(mask):
+        ones = jnp.where(mask, 1.0, 0.0).astype(jnp.bfloat16)
+        return dot_nn(counts, ones)[:1].astype(jnp.int32)
+
+    before = total(first + cap <= row)
+    here = total((first <= row) & (row < first + cap))
+    slot = jnp.bitwise_and(lax.broadcasted_iota(jnp.int32, (1, padded), 1), cap - 1)
+    pos_ref[...] = jnp.where(slot < here, before + slot, -1)
+
     for copy in copies:
         copy.wait()
 
@@ -152,18 +162,23 @@
             t += 1
 
 
-def rows_call(pivot_slots, points, factor):
+def rows_call(pivot_slots, pivot_counts, points, factor):
     cap = pivot_slots.shape[1]
     features, held = points.shape[1], factor.shape[1]
+    counts = pivot_counts.reshape(1, -1)
     return pl.pallas_call(
         rows_kernel,
-        out_shape=jax.ShapeDtypeStruct(((features + held) // 128, cap, 128), jnp.bfloat16),
+        out_shape=(
+            jax.ShapeDtypeStruct(((features + held) // 128, cap, 128), jnp.bfloat16),
+            jax.ShapeDtypeStruct((1, counts.shape[1] * cap), jnp.int32),
+        ),
         in_specs=[
             pl.BlockSpec(memory_space=pltpu.SMEM),
+            pl.BlockSpec(memory_space=pltpu.VMEM),
             pl.BlockSpec(memory_space=pl.ANY),
             pl.BlockSpec(memory_space=pl.ANY),
         ],
-        out_specs=pl.BlockSpec(memory_space=pltpu.VMEM),
+        out_specs=[pl.BlockSpec(memory_space=pltpu.VMEM)] * 2,
         scratch_shapes=[
             pltpu.VMEM((cap, SUB, features), jnp.bfloat16),
             pltpu.VMEM((cap, SUB, held), jnp.bfloat16),
@@ -172,7 +187,7 @@
         ],
         compiler_params=pltpu.CompilerParams(vmem_limit_bytes=ROWS_VMEM),
         name="pivot_rows",
-    )(pivot_slots, points, factor)
+    )(pivot_slots, counts, points, factor)
 
 
 SPANS = ((0, 4, 7), (7, 11, 14), (14, 17, 20))
@@ -773,9 +788,8 @@
 
 
 def on_device(points, factor, targets, pivot_slots, pivot_counts):
-    own = rows_call(pivot_slots, points, factor)
+    own, positions = rows_call(pivot_slots, pivot_counts, points, factor)
     padded, shard = gather_call(own, targets, factor)
-    positions = padded_positions(pivot_counts, pivot_slots.shape[1])
     new_columns, cross, norms = local_call(padded, positions, points, factor, targets)
     coef, fit = sums_call(shard, cross, norms, factor, targets.shape[1])
     residual_next = residual_call(new_columns, targets, fit, coef)

time: 91.7 us -> 91.1 us (level)
  no operation moved by 1% of the time
where the time goes in v7:
time: 91.1 us; the launch traced here: 90.9 us
  Pallas kernels  89.3 us (98%)
    pallas_call x1, Pallas kernels, gather_call(): pl.pallas_call(gather_kernel, out_shape=(jax.ShapeDtypeStruct((4, 2, 4, 4...  33 us
    pallas_call x1, Pallas kernels, local_call(): pl.pallas_call(local_kernel, out_shape=(jax.ShapeDtypeStruct((BLOCK, pts)...  29.4 us
    pallas_call x1, Pallas kernels, sums_call(): pl.pallas_call(sums_kernel, out_shape=(jax.ShapeDtypeStruct((2, fresh, 16...  21.1 us
    pallas_call x1, Pallas kernels, residual_call(): pl.pallas_call(residual_kernel, grid=(pts // TILE_PTS,), out_shape=jax.Sh...  3.07 us
    pallas_call x1, Pallas kernels, rows_call(): pl.pallas_call(rows_kernel, out_shape=(jax.ShapeDtypeStruct(((features +...  2.73 us

profile of v7, /device:TPU:1, one launch (start us, length us, event | category | flops | bytes accessed | tf_op | source)
XLA Modules:
  0.0 90.9 jit_solution(220789711746829568)
XLA Ops:
  0.6 0.0 copy-start
  0.6 2.7 %pivot_rows.1 = (bf16[20,8,128]{2,1,0:T(8,128)(2,1)}, s32[1,1024]{1,0:T(1,128)}) custom-call(s32[1,8]{1,0:T(1,128)} %slots_ref.1, s32[1,128]{1,0:T(1,128)} %bitcast.5, bf16[2048,512]{1,0:T(8,128)(2,1)} %points_ref.3, bf16[2048,2048]{1,0:T(8,128)(2,1)} %factor_ref.7), custom_call_target="tpu_custom_call" | custom-call | tf_op jit(solution)/shard_map/pivot_rows/pallas_call | solution.py:169
  3.4 0.0 copy-done
  3.4 0.0 copy-start.3
  3.4 0.8 copy-done.3
  4.2 0.0 copy-start.1
  4.2 0.0 copy-start.4
  4.2 33.0 %gather_rows.1 = (bf16[4,2,4,4,20,8,128]{6,5,4,3,2,1,0:T(8,128)(2,1)S(1)}, bf16[8,16,128]{2,1,0:T(8,128)(2,1)S(1)}) custom-call(bf16[20,8,128]{2,1,0:T(8,128)(2,1)S(1)} %copy-done.3, bf16[2048,256]{1,0:T(8,128)(2,1)S(1)} %copy-done, bf16[2048,2048]{1,0:T(8,128)(2,1)} %factor_ref.7), custom_call_target="tpu_custom_call" | custom-call | tf_op jit(solution)/shard_map/gather_rows/pallas_call | solution.py:390
  37.1 0.0 slice-start
  37.2 0.0 copy-done.1
  37.2 0.0 copy-done.4
  37.2 0.0 slice-start.1
  37.2 29.4 %local_block.1 = (bf16[512,2048]{1,0:T(8,128)(2,1)}, bf16[2,32,16,128]{3,2,1,0:T(8,128)(2,1)S(1)}, f32[4,128]{1,0:T(4,128)S(1)}) custom-call(bf16[128,20,8,128]{3,2,1,0:T(8,128)(2,1)S(1)} %bitcast.4, s32[1,1024]{1,0:T(1,128)S(1)} %copy-done.4, bf16[2048,256]{1,0:T(8,128)(2,1)S(1)} %copy-done, bf16[2048,512]{1,0:T(8,128)(2,1)S(1)} %copy-done.1, ...), custom_call_target="tpu_custom_call" | custom-call | tf_op jit(solution)/shard_map/local_block/pallas_call | solution.py:574
  66.6 0.0 slice-done
  66.6 0.0 slice-done.1
  66.7 0.0 copy-start.2
  66.7 21.1 %sums.1 = (bf16[2,32,16,128]{3,2,1,0:T(8,128)(2,1)S(1)}, f32[2048,256]{1,0:T(8,128)S(1)}) custom-call(bf16[8,16,128]{2,1,0:T(8,128)(2,1)S(1)} %get-tuple-element.15.shard_ref, bf16[2,32,16,128]{3,2,1,0:T(8,128)(2,1)S(1)} %get-tuple-element.16.x_ref, f32[4,128]{1,0:T(4,128)S(1)} %get-tuple-element.17.n_ref, bf16[2048,2048]{1,0:T(8,128)(2,1)S(1)} %bitcast.3), custom_call_target="tpu_custom_call" | custom-call | tf_op jit(solution)/shard_map/sums/pallas_call | solution.py:744
  87.8 0.0 copy-done.2
  87.8 3.1 %residual.1 = f32[2048,256]{1,0:T(8,128)} custom-call(bf16[512,2048]{1,0:T(8,128)(2,1)S(1)} %copy-done.2, bf16[2048,256]{1,0:T(8,128)(2,1)S(1)} %copy-done, f32[2048,256]{1,0:T(8,128)S(1)} %get-tuple-element.18.fit_ref, bf16[2,32,16,128]{3,2,1,0:T(8,128)(2,1)S(1)} %get-tuple-element.19.coef_ref), custom_call_target="tpu_custom_call" | custom-call | tf_op jit(solution)/shard_map/residual/pallas_call | solution.py:774
  (1 shorter events, 0.0 us)
Async XLA Ops:
  0.6 2.8 %copy-start = (bf16[2048,256]{1,0:T(8,128)(2,1)S(1)}, bf16[2048,256]{1,0:T(8,128)(2,1)}, u32[]{:S(2)}) copy-start(bf16[2048,256]{1,0:T(8,128)(2,1)} %targets_ref.5) | copy-start | bytes 3145732
  3.4 0.8 copy-start.3
  4.2 33.0 %copy-start.1 = (bf16[2048,512]{1,0:T(8,128)(2,1)S(1)}, bf16[2048,512]{1,0:T(8,128)(2,1)}, u32[]{:S(2)}) copy-start(bf16[2048,512]{1,0:T(8,128)(2,1)} %points_ref.3) | copy-start | bytes 6291460
  4.2 33.0 %copy-start.4 = (s32[1,1024]{1,0:T(1,128)S(1)}, s32[1,1024]{1,0:T(1,128)}, u32[]{:S(2)}) copy-start(s32[1,1024]{1,0:T(1,128)} %get-tuple-element.13.pos_ref) | copy-start | bytes 12292
  37.1 29.5 %slice-start = ((s8[8388608]{0:T(1024)(128)(4,1)}), s8[4194304]{0:T(1024)(128)(4,1)S(1)}, s32[]{:S(2)}) async-start(s8[8388608]{0:T(1024)(128)(4,1)} %bitcast.2), calls=%async_computation | async-start | bytes 8388608
  37.2 29.5 %slice-start.1 = ((s8[8388608]{0:T(1024)(128)(4,1)}), s8[4194304]{0:T(1024)(128)(4,1)S(1)}, s32[]{:S(2)}) async-start(s8[8388608]{0:T(1024)(128)(4,1)} %bitcast.2), calls=%async_computation.1 | async-start | bytes 8388608
  66.7 21.2 %copy-start.2 = (bf16[512,2048]{1,0:T(8,128)(2,1)S(1)}, bf16[512,2048]{1,0:T(8,128)(2,1)}, u32[]{:S(2)}) copy-start(bf16[512,2048]{1,0:T(8,128)(2,1)} %get-tuple-element.9.new_ref) | copy-start | bytes 6291460
